TPU v7x, 32 devices: a whole 2x2x4 slice. The times are simulated.
32 devices in a mesh: tr: 4 (over z), tc: 8 (over y, x, core).
Axes of the slice: x: 2, y: 2, z: 4, core: 2. Of those that a mesh axis runs over, the one named last changes fastest.
Arguments:
- cov_tiles: float32 [16384, 16384], P('tr', 'tc'), may hold values from -3 to 9, as said below
- block_order: int32 [32], replicated, may hold values from 0 to 31, as said below
- stations: int32 [1, 256], P(None, 'tc'), may hold values from 0 to 31
- obs_values: float32 [1, 256, 512], P(None, 'tc'), may hold values from -0.25 to 0.25
- obs_error: float32 [1, 256], P(None, 'tc'), may hold values from 0.5 to 4
Outputs:
- cov_updated: float32 [16384, 16384], P('tr', 'tc')
Inputs may be any that keep to these rules, and one draw needn't show every extreme that they name: `block_order`: a permutation of 0 to 31. `cov_tiles`: the matrix that the live tiles describe, completed by symmetry, is positive definite with diagonal tiles symmetric; tiles that are not live are zero.
All inputs are finite; a program needn't handle non-finite values.
Results may differ from a plain program's by a relative error of at most 0.0001.
Values sent between devices are 32-bit elements; how exact they have to be, the bound alone decides.
A program may use at most 192 MiB of HBM per device.

v0:
```python
import jax
import jax.numpy as jnp
from jax import lax
from jax.experimental import pallas as pl
from jax.experimental.pallas import tpu as pltpu
from jax.sharding import PartitionSpec as P

exact = lax.Precision.HIGHEST
quick = lax.Precision.HIGH


def product(former, latter, over, precision=exact):
    return lax.dot_general(
        former,
        latter,
        (((over[0],), (over[1],)), ((), ())),
        precision=precision,
        preferred_element_type=jnp.float32,
    )


def tile_spread(blockwise, tile_size):
    row_count, col_count = blockwise.shape
    return jnp.broadcast_to(
        blockwise[:, None, :, None], (row_count, tile_size, col_count, tile_size)
    ).reshape(row_count * tile_size, col_count * tile_size)


def design_block(order_part, station_codes, values):
    select = (station_codes[None, :] == order_part[:, None]).astype(jnp.float32)
    return (select[:, None, :] * values.T[None, :, :]).reshape(
        order_part.shape[0] * values.shape[1], values.shape[0]
    )


def swept(matrix, work):
    size = matrix.shape[0]
    work[...] = matrix
    lanes = lax.broadcasted_iota(jnp.int32, (1, size), 1)
    rows = lax.broadcasted_iota(jnp.int32, (size, 1), 0)

    def step(pivot, carry):
        held = work[...]
        row = work[pl.ds(pivot, 1), :]
        at_lane = lanes == pivot
        at_row = rows == pivot
        column = jnp.sum(jnp.where(at_lane, held, 0.0), axis=1, keepdims=True)
        share = 1.0 / jnp.sum(jnp.where(at_lane, row, 0.0), axis=1, keepdims=True)
        kept = jnp.where(at_lane | at_row, 0.0, held)
        left = jnp.where(at_row, -1.0, column)
        right = jnp.where(at_lane, -1.0, row)
        work[...] = kept - left * (right * share)
        return carry

    lax.fori_loop(0, size, step, 0)
    return -work[...]


def inverse_of(matrix, work):
    size = matrix.shape[0]
    if size <= 128:
        return swept(matrix, work)
    half = size // 2
    upper, corner, lower = matrix[:half, :half], matrix[half:, :half], matrix[half:, half:]
    upper_inverse = inverse_of(upper, work)
    weight = product(corner, upper_inverse, (1, 0))
    lower_inverse = inverse_of(lower - product(weight, corner, (1, 1)), work)
    below = -product(lower_inverse, weight, (1, 0))
    above = upper_inverse - product(weight, below, (0, 0))
    return jnp.concatenate(
        (jnp.concatenate((above, below.T), axis=1), jnp.concatenate((below, lower_inverse), axis=1)), axis=0
    )


def inverse_kernel(matrix_ref, inverse_ref, work):
    inverse_ref[...] = inverse_of(matrix_ref[...], work)


def inverse(matrix):
    size = matrix.shape[0]
    part = size
    while part > 128:
        part //= 2
    return pl.pallas_call(
        inverse_kernel,
        out_shape=jax.ShapeDtypeStruct(matrix.shape, jnp.float32),
        in_specs=[pl.BlockSpec(memory_space=pltpu.VMEM)],
        out_specs=pl.BlockSpec(memory_space=pltpu.VMEM),
        scratch_shapes=[pltpu.VMEM((part, part), jnp.float32)],
        cost_estimate=pl.CostEstimate(flops=400_000_000, bytes_accessed=8 * size * size, transcendentals=0),
        name="inverse",
    )(matrix)


def body(cov_tiles, block_order, stations, obs_values, obs_error):
    row_rows, col_rows = cov_tiles.shape
    tile_size = obs_values.shape[2]
    row_blocks = row_rows // tile_size
    col_blocks = col_rows // tile_size
    tr_size, tc_size = lax.axis_size("tr"), lax.axis_size("tc")
    row_index = lax.axis_index("tr")
    col_index = lax.axis_index("tc")
    values = lax.all_gather(obs_values[0], "tc", axis=0, tiled=True)
    small = jnp.stack((stations[0].astype(jnp.float32), obs_error[0]))
    small = lax.all_gather(small, "tc", axis=1, tiled=True)
    station_codes, errors = small[0].astype(jnp.int32), small[1]
    row_order = lax.dynamic_slice_in_dim(block_order, row_index * row_blocks, row_blocks)
    col_order = lax.dynamic_slice_in_dim(block_order, col_index * col_blocks, col_blocks)
    row_places = row_index * row_blocks + jnp.arange(row_blocks, dtype=jnp.int32)
    col_places = col_index * col_blocks + jnp.arange(col_blocks, dtype=jnp.int32)
    below_mask = (row_order[:, None] > col_order[None, :]).astype(jnp.float32)
    on_diagonal = (row_places[:, None] == col_places[None, :]).astype(jnp.float32)
    below_full = tile_spread(below_mask, tile_size)
    keep_full = tile_spread(below_mask + on_diagonal, tile_size)
    strict_part = cov_tiles * below_full
    design_rows = design_block(row_order, station_codes, values)
    design_cols = design_block(col_order, station_codes, values)
    row_part = product(cov_tiles, design_cols, (1, 0), quick)
    col_part = product(strict_part, design_rows, (0, 0), quick)
    gram_part = product(design_rows, row_part, (0, 0)) + product(design_cols, col_part, (0, 0))
    innovation = lax.psum(gram_part, ("tr", "tc")) + jnp.diag(errors)
    count = tr_size * tc_size
    to_rows = [((q % tr_size) * tc_size + q // tr_size, q) for q in range(count)]
    to_cols = [(there, here) for here, there in to_rows]
    col_chunk = lax.psum_scatter(col_part, "tr", scatter_dimension=0, tiled=True)
    row_chunk = lax.psum_scatter(row_part, "tc", scatter_dimension=0, tiled=True)
    chunk = row_chunk + lax.ppermute(col_chunk, ("tr", "tc"), to_rows)
    cross_rows = lax.all_gather(chunk, "tc", axis=0, tiled=True)
    cross_cols = lax.all_gather(lax.ppermute(chunk, ("tr", "tc"), to_cols), "tr", axis=0, tiled=True)
    weighted_cols = product(cross_cols, inverse(innovation), (1, 0))
    return (cov_tiles - product(cross_rows, weighted_cols, (1, 1), quick)) * keep_full


def solution(mesh):
    in_specs = (P("tr", "tc"), P(), P(None, "tc"), P(None, "tc", None), P(None, "tc"))
    out_specs = P("tr", "tc")
    return jax.shard_map(body, mesh=mesh, in_specs=in_specs, out_specs=out_specs, check_vma=False)
```

profile of v0, /device:TPU:0, one launch (start us, length us, event | category | flops | bytes accessed | tf_op | source)
XLA Modules:
  0.0 463.8 jit_solution(12726905374221606165)
XLA Ops:
  8.9 11.3 %broadcast_in_dim.19 = f32[8,512,4,512]{3,2,1,0:T(4,128)} broadcast(f32[8,4]{1,0:T(8,128)S(1)} %compare_convert_fusion.1), dimensions={0,2} | broadcast | bytes 33554560 | tf_op jit(solution)/shard_map/broadcast_in_dim | solution.py:24
  20.2 30.0 %copy.17 = f32[512,8,4,512]{3,1,2,0:T(8,128)} copy(f32[512,8,4,512]{3,2,1,0:T(4,128)} %bitcast.34) | data formatting | bytes 67108864
  50.2 10.4 %all-gather.1 = f32[8,32,2]{1,2,0:T(2,128)S(1)} all-gather(f32[1,32,2]{1,2,0:T(2,128)S(1)} %maximum_bitcast_fusion), channel_id=1, replica_groups=mesh['tr'=4,'tc'=8] {'tc'}, dimensions={0}, use_global_device_ids=true | all-gather | bytes 2304 | tf_op jit(solution)/shard_map/all_gather | solution.py:105
  60.8 9.8 %all-gather = f32[1,256,512]{2,1,0:T(8,128)S(1)} all-gather(f32[1,32,512]{2,1,0:T(8,128)S(1)} %copy-done.2), channel_id=2, replica_groups=mesh['tr'=4,'tc'=8] {'tc'}, dimensions={1}, use_global_device_ids=true | all-gather | bytes 589824 | tf_op jit(solution)/shard_map/all_gather | solution.py:103
  70.8 2.4 broadcast_multiply_fusion
  73.2 34.1 %fusion = f32[2048,256]{1,0:T(8,128)S(1)} fusion(f32[4096,256]{1,0:T(8,128)} %bitcast.36, f32[4096,2048]{1,0:T(8,128)} %param.5, f32[4096,2048]{1,0:T(8,128)} %bitcast.32), kind=kOutput, calls=%fused_computation.1 | convolution fusion | flops 12893290496 | bytes 73400320 | tf_op jit(solution)/shard_map/dot_general | solution.py:13
  107.4 1.8 copy.16
  109.5 1.5 broadcast_multiply_fusion.1
  111.0 31.9 %fusion.3 = f32[256,4096]{1,0:T(8,128)} fusion(f32[2048,256]{1,0:T(8,128)} %bitcast.39, f32[4096,2048]{1,0:T(8,128)} %param.5), kind=kOutput, calls=%fused_computation.17 | convolution fusion | flops 12884901888 | bytes 39845888 | tf_op jit(solution)/shard_map/dot_general | solution.py:13
  143.0 10.3 %reduce-scatter.5.cloned.1.call-done = f32[512,256]{0,1:T(8,128)} async-done(((f32[2048,256]{0,1:T(8,128)}), f32[512,256]{0,1:T(8,128)}) %reduce-scatter.5.cloned.1.call-update) | async-done | bytes 524304 | tf_op jit(solution)/shard_map/reduce_scatter | solution.py:125
  153.3 1.7 collective-permute-start
  155.0 5.1 %fusion.4 = f32[256,256]{1,0:T(8,128)S(1)} fusion(f32[2048,256]{1,0:T(8,128)} %bitcast.40, f32[2048,256]{1,0:T(8,128)S(1)} %fusion), kind=kOutput, calls=%fused_computation.18 | convolution fusion | flops 1610612736 | bytes 4456448 | tf_op jit(solution)/shard_map/dot_general | solution.py:13
  160.0 52.5 %reduce-scatter.3.cloned.1.call-done = f32[512,256]{0,1:T(8,128)} async-done(((f32[4096,256]{0,1:T(8,128)}), f32[512,256]{0,1:T(8,128)}) %reduce-scatter.3.cloned.1.call-update) | async-done | bytes 524304 | tf_op jit(solution)/shard_map/reduce_scatter | solution.py:126
  212.6 1.1 add.50
  213.7 0.9 collective-permute-start.1
  214.6 10.9 %convolution_add_fusion = f32[256,256]{1,0:T(8,128)} fusion(f32[256,256]{1,0:T(8,128)S(1)} %fusion.4, f32[4096,256]{1,0:T(8,128)} %bitcast.37, f32[256,4096]{1,0:T(8,128)} %fusion.3), kind=kOutput, calls=%fused_computation.4 | convolution fusion | flops 3221291008 | bytes 8912896 | tf_op jit(solution)/shard_map/dot_general | solution.py:13
  225.6 0.8 copy-done.1
  227.1 11.3 %broadcast_in_dim.23 = f32[8,512,4,512]{3,2,1,0:T(4,128)} broadcast(f32[8,4]{1,0:T(8,128)S(1)} %convert_add_fusion), dimensions={0,2} | broadcast | bytes 33554560 | tf_op jit(solution)/shard_map/broadcast_in_dim | solution.py:24
  238.4 30.2 %copy.18 = f32[512,8,4,512]{3,1,2,0:T(8,128)} copy(f32[512,8,4,512]{3,2,1,0:T(4,128)} %bitcast.35) | data formatting | bytes 67108864
  268.6 110.6 %all-reduce.2.cloned.1.call-done = f32[256,256]{1,0:T(8,128)} async-done(((f32[256,256]{1,0:T(8,128)}), f32[256,256]{1,0:T(8,128)}) %all-reduce.2.cloned.1.call-update) | async-done | bytes 262160 | tf_op jit(solution)/shard_map/psum | solution.py:121
  379.2 1.8 select_add_fusion.matrix_ref
  381.0 27.6 %inverse.1 = f32[256,256]{1,0:T(8,128)} custom-call(f32[256,256]{1,0:T(8,128)} %select_add_fusion.matrix_ref), custom_call_target="tpu_custom_call" | custom-call | flops 400000000 | bytes 524288 | tf_op jit(solution)/shard_map/inverse/pallas_call | solution.py:84
  408.6 5.0 %fusion.5 = f32[2048,256]{1,0:T(8,128)S(1)} fusion(f32[2048,256]{0,1:T(8,128)} %all-gather.7.cloned.1.call-done, f32[256,256]{1,0:T(8,128)} %inverse.1), kind=kOutput, calls=%fused_computation.19 | convolution fusion | flops 1610612736 | bytes 4456448 | tf_op jit(solution)/shard_map/dot_general | solution.py:13
  413.6 42.6 %subtract_multiply_fusion = f32[4096,2048]{1,0:T(8,128)} fusion(f32[4096,2048]{1,0:T(8,128)} %bitcast.33, f32[4096,2048]{1,0:T(8,128)} %param.5, f32[4096,256]{0,1:T(8,128)} %all-gather.5.cloned.1.call-done, f32[2048,256]{1,0:T(8,128)S(1)} %fusion.5), kind=kOutput, calls=%fused_computation | convolution fusion | flops 12901679104 | bytes 106954752 | tf_op jit(solution)/shard_map/dot_general | solution.py:13
  (37 shorter events, 3.0 us)
Async XLA Ops:
  7.4 145.9 %reduce-scatter.5.cloned.1.call-start = ((), (), s32[]{:S(2)}) async-start(), calls=%async_computation.3 | async-start | bytes 2621440 | tf_op jit(solution)/shard_map/reduce_scatter | solution.py:125
  20.2 30.0 %copy-start.4 = (s32[1,32]{1,0:T(1,128)S(1)}, s32[1,32]{1,0:T(1,128)}, u32[]{:S(2)}) copy-start(s32[1,32]{1,0:T(1,128)} %param.7) | copy-start | bytes 388
  20.2 30.0 %copy-start.3 = (f32[1,32]{1,0:T(1,128)S(1)}, f32[1,32]{1,0:T(1,128)}, u32[]{:S(2)}) copy-start(f32[1,32]{1,0:T(1,128)} %param.9) | copy-start | bytes 388
  20.2 40.6 %copy-start.2 = (f32[1,32,512]{2,1,0:T(8,128)S(1)}, f32[1,32,512]{2,1,0:T(8,128)}, u32[]{:S(2)}) copy-start(f32[1,32,512]{2,1,0:T(8,128)} %param.8) | copy-start | bytes 196612
  109.2 103.3 %reduce-scatter.3.cloned.1.call-start = ((), (), s32[]{:S(2)}) async-start(), calls=%async_computation.2 | async-start | bytes 4718592 | tf_op jit(solution)/shard_map/reduce_scatter | solution.py:126
  142.9 236.3 %all-reduce.2.cloned.1.call-start = ((), (), s32[]{:S(2)}) async-start(), calls=%async_computation.6 | async-start | bytes 524288 | tf_op jit(solution)/shard_map/psum | solution.py:121
  153.3 6.8 %collective-permute-start = (f32[512,256]{0,1:T(8,128)}, f32[512,256]{0,1:T(8,128)S(1)}, u32[]{:S(2)}, u32[]{:S(2)}) collective-permute-start(f32[512,256]{0,1:T(8,128)} %reduce-scatter.5.cloned.1.call-done), channel_id=1, source_target_pairs={{0,0},{8,1},{16,2},{24,3},{1,4},{9,5},{17,6},{25,7},{2,8},{10,9},{... | collective-permute-start | bytes 1572872 | tf_op jit(solution)/shard_map/ppermute | solution.py:127
  213.7 11.8 %copy-start = (f32[512,256]{0,1:T(8,128)}, f32[512,256]{0,1:T(8,128)S(1)}, u32[]{:S(2)}) copy-start(f32[512,256]{0,1:T(8,128)S(1)} %add.50) | copy-start | bytes 1572868
  213.7 11.9 %collective-permute-start.1 = (f32[512,256]{0,1:T(8,128)S(1)}, f32[512,256]{0,1:T(8,128)S(1)}, u32[]{:S(2)}, u32[]{:S(2)}) collective-permute-start(f32[512,256]{0,1:T(8,128)S(1)} %add.50), channel_id=1, source_target_pairs={{0,0},{1,8},{2,16},{3,24},{4,1},{5,9},{6,17},{7,25},{8,2},{9,10},{... | collective-permute-start | bytes 1572872 | tf_op jit(solution)/shard_map/ppermute | solution.py:129
  225.6 183.0 %all-gather.7.cloned.1.call-start = ((), (), s32[]{:S(2)}) async-start(), calls=%async_computation.5 | async-start | bytes 2621440 | tf_op jit(solution)/shard_map/all_gather | solution.py:129
  225.6 0.8 copy-start.1
  226.5 187.2 %all-gather.5.cloned.1.call-start = ((), (), s32[]{:S(2)}) async-start(), calls=%async_computation.4 | async-start | bytes 4718592 | tf_op jit(solution)/shard_map/all_gather | solution.py:128
Sparse Core Ops, SparseCore 0:
  109.4 43.8 reduce-scatter.4
  156.6 55.9 reduce-scatter.2
  228.0 60.9 all-gather.6
  290.7 35.5 all-gather.4
Sparse Core Ops, SparseCore 1:
  225.7 153.5 all-reduce.1
where the time goes:
time: 473 us; the launch traced here: 464 us
  waiting for transfers between devices  174 us (37%)
  matrix products  130 us (27%)
  local copies, waits for them, and re-layouts  87.1 us (18%)
  Pallas kernels  27.6 us (6%)
  blocking collectives  20.2 us (4%)
  between operations  15.2 us (3%)
  other arithmetic  7.11 us (2%)
    dot_general x6, matrix products, product(): lax.dot_general(former, latter, (((over[0],), (over[1],)), ((), ())), pre...  130 us
    psum x1, waiting for transfers between devices, body(): innovation = lax.psum(gram_part, ('tr', 'tc')) + jnp.diag(errors)  111 us
    unnamed x13, local copies, waits for them, and re-layouts  61.1 us
    reduce_scatter x1, waiting for transfers between devices, body(): lax.psum_scatter(row_part, 'tc', scatter_dimension=0, tiled=True)  52.5 us
    pallas_call x1, Pallas kernels, inverse(): pl.pallas_call(inverse_kernel, out_shape=jax.ShapeDtypeStruct(matrix.shap...  27.6 us
    broadcast_in_dim x2, local copies, waits for them, and re-layouts, tile_spread(): jnp.broadcast_to(blockwise[:, None, :, None], (row_count, tile_size, col_...  22.6 us
    all_gather x1, blocking collectives, body(): small = lax.all_gather(small, 'tc', axis=1, tiled=True)  10.4 us
    reduce_scatter x1, waiting for transfers between devices, body(): lax.psum_scatter(col_part, 'tr', scatter_dimension=0, tiled=True)  10.3 us
  transfers between devices with their start and end apart: 7, of which 3 were waited for; matrix products, arithmetic and copies ran while one was open for 21% of the time, Pallas kernels for 6%

commit v1 on v0

v1 whole, which is shorter than its diff:
```python
import functools

import jax
import jax.numpy as jnp
from jax import lax
from jax.experimental import pallas as pl
from jax.experimental.pallas import tpu as pltpu
from jax.sharding import PartitionSpec as P

exact = lax.Precision.HIGHEST
bf16, f32, i32 = jnp.bfloat16, jnp.float32, jnp.int32
DEPTH = 4
ANY = pl.BlockSpec(memory_space=pl.ANY)
VMEM = pl.BlockSpec(memory_space=pltpu.VMEM)
SMEM = pl.BlockSpec(memory_space=pltpu.SMEM)


def product(former, latter, over, precision=exact):
    return lax.dot_general(
        former,
        latter,
        (((over[0],), (over[1],)), ((), ())),
        precision=precision,
        preferred_element_type=jnp.float32,
    )


def halves(array):
    high = array.astype(bf16)
    return high, (array - high.astype(f32)).astype(bf16)


def dot(former, latter):
    return jnp.dot(former, latter, preferred_element_type=f32)


def dot3(former, latter):
    return dot(former[0], latter[0]) + dot(former[0], latter[1]) + dot(former[1], latter[0])


def list_tiles(order_ref, live_ref, row_blocks, col_blocks, when_dead=None):
    row_first = lax.axis_index("tr") * row_blocks
    col_first = lax.axis_index("tc") * col_blocks

    def step(tile, count):
        row, col = tile // col_blocks, tile % col_blocks
        p, q = row_first + row, col_first + col
        live = (order_ref[p] > order_ref[q]) | (p == q)

        @pl.when(live)
        def _():
            live_ref[count] = tile

        if when_dead is not None:

            @pl.when(jnp.logical_not(live))
            def _():
                when_dead(tile)

        return count + live.astype(i32)

    return lax.fori_loop(0, row_blocks * col_blocks, step, jnp.int32(0))


def tile_at(ref, tile, col_blocks, size):
    row, col = tile // col_blocks, tile % col_blocks
    return ref.at[
        pl.ds(pl.multiple_of(row * size, size), size), pl.ds(pl.multiple_of(col * size, size), size)
    ]


def forward_kernel(
    order_ref, packed_ref, cov_ref, rows_ref, cols_ref, gram_ref,
    live_ref, held, sem, for_rows, for_cols,
):
    row_blocks, size, count_obs = rows_ref.shape
    col_blocks = cols_ref.shape[0]
    row_first = lax.axis_index("tr") * row_blocks
    col_first = lax.axis_index("tc") * col_blocks
    count = list_tiles(order_ref, live_ref, row_blocks, col_blocks)

    def fetch(at):
        slot = at % DEPTH
        return pltpu.make_async_copy(
            tile_at(cov_ref, live_ref[at], col_blocks, size), held.at[slot], sem.at[slot]
        )

    for at in range(DEPTH - 1):

        @pl.when(at < count)
        def _():
            fetch(at).start()

    values = packed_ref[:, :size]
    extras = packed_ref[:, size:]
    codes_down = extras[:, 0:1].astype(i32)
    flipped = extras.T
    codes_across = flipped[0:1, :].astype(i32)
    errors_across = flipped[1:2, :]
    values_t = values.T
    for block in range(row_blocks):
        chosen = jnp.where(codes_down == order_ref[row_first + block], values, 0.0)
        for_rows[block, 0], for_rows[block, 1] = halves(chosen)
    for block in range(col_blocks):
        chosen = jnp.where(codes_across == order_ref[col_first + block], values_t, 0.0)
        for_cols[block, 0], for_cols[block, 1] = halves(chosen)
    rows_ref[...] = jnp.zeros_like(rows_ref)
    cols_ref[...] = jnp.zeros_like(cols_ref)

    def step(at, carry):
        tile = live_ref[at]
        row, col = tile // col_blocks, tile % col_blocks
        slot = at % DEPTH

        @pl.when(at + DEPTH - 1 < count)
        def _():
            fetch(at + DEPTH - 1).start()

        fetch(at).wait()
        parts = halves(held[slot])
        rows_ref[row] += dot3(parts, (for_cols[col, 0], for_cols[col, 1]))

        @pl.when(row_first + row != col_first + col)
        def _():
            cols_ref[col] += dot3((for_rows[row, 0], for_rows[row, 1]), parts)

        return carry

    lax.fori_loop(0, count, step, 0)
    first = (lax.axis_index("tr") == 0) & (lax.axis_index("tc") == 0)
    across = lax.broadcasted_iota(i32, (count_obs, count_obs), 1)
    down = lax.broadcasted_iota(i32, (count_obs, count_obs), 0)
    gram_ref[...] = jnp.zeros_like(gram_ref)

    def add_col(block, carry):
        gram_ref[...] += dot3(halves(cols_ref[block]), (for_cols[block, 0], for_cols[block, 1]))
        return carry

    lax.fori_loop(0, col_blocks, add_col, 0)
    gram_ref[...] = gram_ref[...].T + jnp.where((across == down) & first, errors_across, 0.0)

    def add_row(block, carry):
        gram_ref[...] += dot3((for_rows[block, 0], for_rows[block, 1]), halves(rows_ref[block]))
        return carry

    lax.fori_loop(0, row_blocks, add_row, 0)


def forward(block_order, packed, cov_tiles, size):
    count_obs = packed.shape[0]
    row_blocks, col_blocks = cov_tiles.shape[0] // size, cov_tiles.shape[1] // size
    tiles = row_blocks * col_blocks
    return pl.pallas_call(
        forward_kernel,
        out_shape=(
            jax.ShapeDtypeStruct((row_blocks, size, count_obs), f32),
            jax.ShapeDtypeStruct((col_blocks, count_obs, size), f32),
            jax.ShapeDtypeStruct((count_obs, count_obs), f32),
        ),
        in_specs=[SMEM, VMEM, ANY],
        out_specs=(VMEM, VMEM, VMEM),
        scratch_shapes=[
            pltpu.SMEM((tiles,), i32),
            pltpu.VMEM((DEPTH, size, size), f32),
            pltpu.SemaphoreType.DMA((DEPTH,)),
            pltpu.VMEM((row_blocks, 2, count_obs, size), bf16),
            pltpu.VMEM((col_blocks, 2, size, count_obs), bf16),
        ],
        cost_estimate=pl.CostEstimate(
            flops=6 * tiles * size * size * count_obs, bytes_accessed=2 * tiles * size * size, transcendentals=0
        ),
        name="forward",
    )(block_order, packed, cov_tiles)


def update_kernel(
    order_ref, rows_ref, cols_ref, inverse_ref, cov_ref, out_ref,
    live_ref, held, made, zeros, weighted, in_sem, out_sem, zero_sem,
):
    row_blocks, size, _ = rows_ref.shape
    col_blocks = cols_ref.shape[0]
    tiles = row_blocks * col_blocks
    zeros[...] = jnp.zeros_like(zeros)

    def blank(tile):
        return pltpu.make_async_copy(zeros, tile_at(out_ref, tile, col_blocks, size), zero_sem.at[tile])

    count = list_tiles(order_ref, live_ref, row_blocks, col_blocks)

    def fetch(at):
        slot = at % DEPTH
        return pltpu.make_async_copy(
            tile_at(cov_ref, live_ref[at], col_blocks, size), held.at[slot], in_sem.at[slot]
        )

    def put(at):
        slot = at % DEPTH
        return pltpu.make_async_copy(
            made.at[slot], tile_at(out_ref, live_ref[at], col_blocks, size), out_sem.at[slot]
        )

    for at in range(DEPTH - 1):

        @pl.when(at < count)
        def _():
            fetch(at).start()

    list_tiles(order_ref, live_ref, row_blocks, col_blocks, lambda tile: blank(tile).start())
    for block in range(col_blocks):
        weighted[block, 0], weighted[block, 1] = halves(product(inverse_ref[...], cols_ref[block], (1, 0)))

    def step(at, carry):
        tile = live_ref[at]
        row, col = tile // col_blocks, tile % col_blocks
        slot = at % DEPTH

        @pl.when(at + DEPTH - 1 < count)
        def _():
            fetch(at + DEPTH - 1).start()

        @pl.when(at >= DEPTH)
        def _():
            put(at - DEPTH).wait()

        fetch(at).wait()
        made[slot] = held[slot] - dot3(halves(rows_ref[row]), (weighted[col, 0], weighted[col, 1]))
        put(at).start()
        return carry

    lax.fori_loop(0, count, step, 0)
    lax.fori_loop(jnp.maximum(count - DEPTH, 0), count, lambda at, carry: (put(at).wait(), carry)[1], 0)
    list_tiles(order_ref, live_ref, row_blocks, col_blocks, lambda tile: blank(tile).wait())


def update(block_order, cross_rows, cross_cols, inverted, cov_tiles):
    row_blocks, size, count_obs = cross_rows.shape
    col_blocks = cross_cols.shape[0]
    tiles = row_blocks * col_blocks
    return pl.pallas_call(
        update_kernel,
        out_shape=jax.ShapeDtypeStruct(cov_tiles.shape, f32),
        in_specs=[SMEM, VMEM, VMEM, VMEM, ANY],
        out_specs=ANY,
        scratch_shapes=[
            pltpu.SMEM((tiles,), i32),
            pltpu.VMEM((DEPTH, size, size), f32),
            pltpu.VMEM((DEPTH, size, size), f32),
            pltpu.VMEM((size, size), f32),
            pltpu.VMEM((col_blocks, 2, count_obs, size), bf16),
            pltpu.SemaphoreType.DMA((DEPTH,)),
            pltpu.SemaphoreType.DMA((DEPTH,)),
            pltpu.SemaphoreType.DMA((tiles,)),
        ],
        cost_estimate=pl.CostEstimate(
            flops=3 * tiles * size * size * count_obs, bytes_accessed=6 * tiles * size * size, transcendentals=0
        ),
        name="update",
    )(block_order, cross_rows, cross_cols, inverted, cov_tiles)


def swept(matrix, work):
    size = matrix.shape[0]
    work[...] = matrix
    lanes = lax.broadcasted_iota(jnp.int32, (1, size), 1)
    rows = lax.broadcasted_iota(jnp.int32, (size, 1), 0)

    def step(pivot, carry):
        held = work[...]
        row = work[pl.ds(pivot, 1), :]
        at_lane = lanes == pivot
        at_row = rows == pivot
        column = jnp.sum(jnp.where(at_lane, held, 0.0), axis=1, keepdims=True)
        share = 1.0 / jnp.sum(jnp.where(at_lane, row, 0.0), axis=1, keepdims=True)
        kept = jnp.where(at_lane | at_row, 0.0, held)
        left = jnp.where(at_row, -1.0, column)
        right = jnp.where(at_lane, -1.0, row)
        work[...] = kept - left * (right * share)
        return carry

    lax.fori_loop(0, size, step, 0)
    return -work[...]


def inverse_of(matrix, work):
    size = matrix.shape[0]
    if size <= 128:
        return swept(matrix, work)
    half = size // 2
    upper, corner, lower = matrix[:half, :half], matrix[half:, :half], matrix[half:, half:]
    upper_inverse = inverse_of(upper, work)
    weight = product(corner, upper_inverse, (1, 0))
    lower_inverse = inverse_of(lower - product(weight, corner, (1, 1)), work)
    below = -product(lower_inverse, weight, (1, 0))
    above = upper_inverse - product(weight, below, (0, 0))
    return jnp.concatenate(
        (jnp.concatenate((above, below.T), axis=1), jnp.concatenate((below, lower_inverse), axis=1)), axis=0
    )


def inverse_kernel(matrix_ref, inverse_ref, work):
    inverse_ref[...] = inverse_of(matrix_ref[...], work)


def inverse(matrix):
    size = matrix.shape[0]
    part = size
    while part > 128:
        part //= 2
    return pl.pallas_call(
        inverse_kernel,
        out_shape=jax.ShapeDtypeStruct(matrix.shape, jnp.float32),
        in_specs=[pl.BlockSpec(memory_space=pltpu.VMEM)],
        out_specs=pl.BlockSpec(memory_space=pltpu.VMEM),
        scratch_shapes=[pltpu.VMEM((part, part), jnp.float32)],
        cost_estimate=pl.CostEstimate(flops=400_000_000, bytes_accessed=8 * size * size, transcendentals=0),
        name="inverse",
    )(matrix)


def pack(stations, obs_values, obs_error):
    values = obs_values[0]
    count, size = values.shape
    return jnp.concatenate(
        (
            values,
            stations[0].astype(f32)[:, None],
            obs_error[0][:, None],
            jnp.zeros((count, 126), f32),
        ),
        axis=1,
    )


def exchange_plain(row_part, col_part, gram_part):
    tr_size, tc_size = lax.axis_size("tr"), lax.axis_size("tc")
    row_blocks, size, count_obs = row_part.shape
    col_blocks = col_part.shape[0]
    row_part = row_part.reshape(row_blocks * size, count_obs)
    col_part = col_part.transpose(0, 2, 1).reshape(col_blocks * size, count_obs)
    innovation = lax.psum(gram_part, ("tr", "tc"))
    count = tr_size * tc_size
    to_rows = [((q % tr_size) * tc_size + q // tr_size, q) for q in range(count)]
    to_cols = [(there, here) for here, there in to_rows]
    col_chunk = lax.psum_scatter(col_part, "tr", scatter_dimension=0, tiled=True)
    row_chunk = lax.psum_scatter(row_part, "tc", scatter_dimension=0, tiled=True)
    chunk = row_chunk + lax.ppermute(col_chunk, ("tr", "tc"), to_rows)
    cross_rows = lax.all_gather(chunk, "tc", axis=0, tiled=True)
    cross_cols = lax.all_gather(lax.ppermute(chunk, ("tr", "tc"), to_cols), "tr", axis=0, tiled=True)
    return (
        cross_rows.reshape(row_blocks, size, count_obs),
        cross_cols.reshape(col_blocks, size, count_obs).transpose(0, 2, 1),
        innovation,
    )


class Sems:
    def __init__(self):
        self.count = 0

    def take(self, number=1):
        self.count += number
        return self.count - number


def share_kernel(mine_ref, all_ref, send, recv):
    row, col = lax.axis_index("tr"), lax.axis_index("tc")
    many = all_ref.shape[0]
    copies = [
        pltpu.make_async_remote_copy(
            mine_ref, all_ref.at[col], send.at[step], recv.at[step],
            device_id=(row, lax.rem(col + step, many)), device_id_type=pl.DeviceIdType.MESH,
        )
        for step in range(1, many)
    ]
    for copy in copies:
        copy.start()
    all_ref[col] = mine_ref[...]
    for copy in copies:
        copy.wait_send()
    for step in range(1, many):
        pltpu.make_async_remote_copy(
            mine_ref, all_ref.at[lax.rem(col + many - step, many)], send.at[step], recv.at[step],
            device_id=(row, lax.rem(col + step, many)), device_id_type=pl.DeviceIdType.MESH,
        ).wait_recv()


def share(packed):
    many = lax.axis_size("tc")
    full = pl.pallas_call(
        share_kernel,
        out_shape=jax.ShapeDtypeStruct((many, *packed.shape), f32),
        in_specs=[VMEM],
        out_specs=VMEM,
        scratch_shapes=[pltpu.SemaphoreType.DMA((many,)), pltpu.SemaphoreType.DMA((many,))],
        compiler_params=pltpu.CompilerParams(has_side_effects=True),
        name="share",
    )(packed)
    return full.reshape(many * packed.shape[0], packed.shape[1])


def exchange_kernel(
    count_bits, row_ref, col_ref, gram_ref, rows_out, cols_out, gram_out,
    send, recv, from_core, sums, landed, upward, downward, rows_here, cols_here, total,
    gram_work, gram_core, gram_bits, gram_line,
):
    sems = Sems()
    line = lax.axis_size("tr")
    z, j = lax.axis_index("tr"), lax.axis_index("tc")
    chip, core = j // 2, j % 2
    parts = count_bits
    width = rows_here.shape[1]
    pending = []
    beside = (z, 2 * chip + 1 - core)

    def copy(source, target, sem, device=beside):
        return pltpu.make_async_remote_copy(
            source, target, send.at[sem], recv.at[sem], device_id=device, device_id_type=pl.DeviceIdType.MESH
        )

    def begin(source, target, device):
        made = copy(source, target, sems.take(), device)
        made.start()
        pending.append(made)
        return made

    def bit(number):
        return chip // 2**number % 2

    def across(number):
        return z, 2 * (chip + (1 - 2 * bit(number)) * 2**number) + core

    up, down = sems.take(line), sems.take(line)

    def line_begin(step):
        chunk, other = line - step, step - 1

        @pl.when(z == 0)
        def _():
            copy(col_ref.at[chunk], upward.at[chunk], up + chunk, (z + 1, j)).start()

        @pl.when(z == line - 1)
        def _():
            copy(col_ref.at[other], downward.at[other], down + other, (z - 1, j)).start()

    def line_pass(step):
        chunk, other = line - step, step - 1

        @pl.when((z > 0) & (z < chunk))
        def _():
            copy(upward.at[chunk], upward.at[chunk], up + chunk).wait_recv()
            upward[chunk] += col_ref[chunk]
            copy(upward.at[chunk], upward.at[chunk], up + chunk, (z + 1, j)).start()

        @pl.when((z < line - 1) & (z > other))
        def _():
            copy(downward.at[other], downward.at[other], down + other).wait_recv()
            downward[other] += col_ref[other]
            copy(downward.at[other], downward.at[other], down + other, (z - 1, j)).start()

    def line_end():
        total[...] = col_ref[z]

        @pl.when(z > 0)
        def _():
            copy(upward.at[z], upward.at[z], up + z).wait_recv()
            total[...] += upward[z]

        @pl.when(z < line - 1)
        def _():
            copy(downward.at[z], downward.at[z], down + z).wait_recv()
            total[...] += downward[z]

    def line_sent():
        for step in range(1, line):
            chunk, other = line - step, step - 1

            @pl.when(z < chunk)
            def _():
                copy(upward.at[chunk], upward.at[chunk], up + chunk).wait_send()

            @pl.when(z > other)
            def _():
                copy(downward.at[other], downward.at[other], down + other).wait_send()

    def chosen(part, step, flip):
        order = [(part + turn) % count_bits for turn in range(count_bits)]
        free = order[step + 1:]
        picks = []
        for pick in range(2 ** len(free)):
            where = 0
            for turn, number in enumerate(order):
                if number in free:
                    value = pick // 2 ** free.index(number) % 2
                elif turn == step and flip:
                    value = 1 - bit(number)
                else:
                    value = bit(number)
                where = where + value * 2**number
            picks.append(where)
        return order[step], picks

    step_base = [0]
    for step in range(count_bits):
        step_base.append(step_base[-1] + parts * 2 ** (count_bits - 1 - step))

    def plane_send(step):
        made = []
        for part in range(parts):
            number, picks = chosen(part, step, True)
            for slot, pick in enumerate(picks):
                at = step_base[step] + part * len(picks) + slot
                made.append(begin(sums.at[pick, part], landed.at[at], across(number)))
        return made

    def plane_add(step, made):
        for one in made:
            one.wait_recv()
        for part in range(parts):
            _, picks = chosen(part, step, False)
            for slot, pick in enumerate(picks):
                sums[pick, part] += landed[step_base[step] + part * len(picks) + slot]

    line_begin(1)
    held = 2**count_bits
    half = begin(gram_ref.at[pl.ds((1 - core) * held, held)], gram_core, beside)
    core_sum = begin(row_ref.at[1 - core], from_core, beside)
    half.wait_recv()
    gram_work[pl.ds(core * held, held)] = gram_ref[pl.ds(core * held, held)] + gram_core[...]
    for number in reversed(range(count_bits)):
        size = 2**number
        start = core * held + chip // (2 * size) * (2 * size)
        keep, give = start + bit(number) * size, start + (1 - bit(number)) * size
        begin(gram_work.at[pl.ds(give, size)], gram_bits.at[pl.ds(size, size)], across(number)).wait_recv()
        gram_work[pl.ds(keep, size)] += gram_bits[pl.ds(size, size)]
    mine = core * held + chip
    gram_line[z] = gram_work[mine]
    base = sems.take(line)
    for step in range(1, line):
        copy(gram_work.at[mine], gram_line.at[z], base + step, (lax.rem(z + step, line), j)).start()
    for step in range(2, line):
        line_begin(step)

    core_sum.wait_recv()
    sums[...] = row_ref[core] + from_core[...]
    made = plane_send(0)
    for step in range(1, line):
        copy(gram_work.at[mine], gram_line.at[lax.rem(z + line - step, line)], base + step).wait()
    gram_out[mine] = sum(gram_line[step] for step in range(line))
    line_pass(1)
    for number in range(count_bits):
        size = 2**number
        start = core * held + chip // size * size
        begin(gram_out.at[pl.ds(start, size)], gram_out.at[pl.ds(start, size)], across(number)).wait_recv()
    begin(gram_out.at[pl.ds(core * held, held)], gram_out.at[pl.ds(core * held, held)], beside).wait_recv()
    for step in range(1, max(line - 1, count_bits)):
        if step < count_bits:
            plane_add(step - 1, made)
            made = plane_send(step)
        if step + 1 < line - 1:
            line_pass(step + 1)
    plane_add(count_bits - 1, made)

    to_rows, to_cols = sems.take(), sems.take()
    partner = (chip, 2 * z + core)
    apart = z != chip

    @pl.when(apart)
    def _():
        copy(sums.at[chip], rows_here, to_rows, partner).start()

    if line > 2:
        line_pass(line - 1)
    line_end()

    @pl.when(apart)
    def _():
        copy(total, cols_here, to_cols, partner).start()
        copy(sums.at[chip], rows_here, to_rows, partner).wait()

    @pl.when(jnp.logical_not(apart))
    def _():
        rows_here[...] = sums[chip]
        cols_here[...] = total[...]

    for part in range(parts):
        lanes = slice(part * width, (part + 1) * width)
        cols_out[z, :, lanes] = total[:, lanes] + rows_here[part].T
    around, back = sems.take(line), sems.take(line)

    def line_spread(step):
        chunk, other = z - (step - 1), z + (step - 1)

        @pl.when(chunk >= 0)
        def _():
            if step > 1:
                copy(cols_out.at[chunk], cols_out.at[chunk], around + chunk).wait_recv()

            @pl.when(z < line - 1)
            def _():
                copy(cols_out.at[chunk], cols_out.at[chunk], around + chunk, (z + 1, j)).start()

        @pl.when(other < line)
        def _():
            if step > 1:
                copy(cols_out.at[other], cols_out.at[other], back + other).wait_recv()

            @pl.when(z > 0)
            def _():
                copy(cols_out.at[other], cols_out.at[other], back + other, (z - 1, j)).start()

    def line_spread_sent():
        for step in range(1, line + 1):
            chunk, other = z - (step - 1), z + (step - 1)

            @pl.when((chunk >= 0) & (z < line - 1))
            def _():
                copy(cols_out.at[chunk], cols_out.at[chunk], around + chunk).wait_send()

            @pl.when((other < line) & (z > 0))
            def _():
                copy(cols_out.at[other], cols_out.at[other], back + other).wait_send()

    line_spread(1)

    @pl.when(apart)
    def _():
        copy(total, cols_here, to_cols, partner).wait()

    for part in range(parts):
        lanes = slice(part * width, (part + 1) * width)
        rows_out[core, chip, part] = sums[chip, part] + cols_here[:, lanes].T

    made = []
    for turn in range(max(line, count_bits + 1)):
        for one in made:
            one.wait_recv()
        made = []
        if turn < count_bits:
            for part in range(parts):
                number, picks = chosen(part, count_bits - 1 - turn, False)
                for pick in picks:
                    spot = rows_out.at[core, pick, part]
                    made.append(begin(spot, spot, across(number)))
        elif turn == count_bits:
            made = [begin(rows_out.at[core], rows_out.at[core], beside)]
        if 1 <= turn < line:
            line_spread(turn + 1)
    for one in made:
        one.wait_recv()
    line_spread_sent()
    line_sent()
    for one in pending:
        one.wait_send()


def exchange(row_part, col_part, gram_part):
    line, many = lax.axis_size("tr"), lax.axis_size("tc")
    count_bits = line.bit_length() - 1
    row_blocks, size, count_obs = row_part.shape
    parts, width = count_bits, size // count_bits
    seg = count_obs // many
    rows = (2, line, parts, width, count_obs)
    cols = col_part.shape
    gram = (many, seg, count_obs)
    landings = sum(parts * 2 ** (count_bits - 1 - step) for step in range(count_bits))
    cross_rows, cross_cols, innovation = pl.pallas_call(
        functools.partial(exchange_kernel, count_bits),
        out_shape=tuple(jax.ShapeDtypeStruct(shape, f32) for shape in (rows, cols, gram)),
        in_specs=[VMEM] * 3,
        out_specs=(VMEM,) * 3,
        scratch_shapes=[
            pltpu.SemaphoreType.DMA((96,)),
            pltpu.SemaphoreType.DMA((96,)),
            pltpu.VMEM(rows[1:], f32),
            pltpu.VMEM(rows[1:], f32),
            pltpu.VMEM((landings, width, count_obs), f32),
            pltpu.VMEM(cols, f32),
            pltpu.VMEM(cols, f32),
            pltpu.VMEM(rows[2:], f32),
            pltpu.VMEM(cols[1:], f32),
            pltpu.VMEM(cols[1:], f32),
            pltpu.VMEM(gram, f32),
            pltpu.VMEM((many // 2, seg, count_obs), f32),
            pltpu.VMEM((many // 2, seg, count_obs), f32),
            pltpu.VMEM((line, seg, count_obs), f32),
        ],
        compiler_params=pltpu.CompilerParams(has_side_effects=True),
        name="exchange",
    )(row_part.reshape(rows), col_part, gram_part.reshape(gram))
    return cross_rows.reshape(row_part.shape), cross_cols, innovation.reshape(gram_part.shape)


def body(cov_tiles, block_order, stations, obs_values, obs_error):
    size = obs_values.shape[2]
    line, many = lax.axis_size("tr"), lax.axis_size("tc")
    packed = share(pack(stations, obs_values, obs_error))
    row_part, col_part, gram_part = forward(block_order, packed, cov_tiles, size)
    square = many == 2 * line and line & (line - 1) == 0 and line > 1
    whole_tiles = row_part.shape[0] == many and col_part.shape[0] == line
    spread = exchange if square and whole_tiles else exchange_plain
    cross_rows, cross_cols, innovation = spread(row_part, col_part, gram_part)
    return update(block_order, cross_rows, cross_cols, inverse(innovation), cov_tiles)


def solution(mesh):
    in_specs = (P("tr", "tc"), P(), P(None, "tc"), P(None, "tc", None), P(None, "tc"))
    out_specs = P("tr", "tc")
    return jax.shard_map(body, mesh=mesh, in_specs=in_specs, out_specs=out_specs, check_vma=False)
```

time: 473 us -> 279 us (0.59)
  Pallas kernels: 27.6 us -> 271 us
  waiting for transfers between devices: 174 us -> 0 us
  matrix products: 130 us -> 0 us
  local copies, waits for them, and re-layouts: 87.1 us -> 0.9 us
  blocking collectives: 20.2 us -> 0 us
  between operations: 15.2 us -> 0.03 us
  other arithmetic: 7.11 us -> 2.21 us
    pallas_call x0 -> x4, Pallas kernels: none -> 244 us  [the longest x1 171 us: exchange(): pl.pallas_call(functools.partial(exchange_kernel, count_bits), out_shape=...]
    dot_general x6 -> x0, matrix products: 130 us -> none  [product(): lax.dot_general(former, latter, (((over[0],), (over[1],)), ((), ())), pre...]
    psum x1 -> x0, waiting for transfers between devices: 111 us -> none  [body(): innovation = lax.psum(gram_part, ('tr', 'tc')) + jnp.diag(errors)]
    reduce_scatter x2 -> x0, waiting for transfers between devices: 62.9 us -> none  [the longest x1 52.5 us: body(): lax.psum_scatter(row_part, 'tc', scatter_dimension=0, tiled=True)]
    unnamed x13 -> x0, local copies, waits for them, and re-layouts: 61.1 us -> none
    broadcast_in_dim x2 -> x1, local copies, waits for them, and re-layouts: 22.6 us -> 0.01 us  [pack(): jnp.zeros((count, 126), f32)]
    all_gather x2 -> x0, blocking collectives: 20.2 us -> none  [the longest x1 10.4 us: body(): small = lax.all_gather(small, 'tc', axis=1, tiled=True)]
  transfers between devices with their start and end apart: 7 -> 0, of which waited for: 3 -> 0; matrix products, arithmetic and copies ran while one was open for 21% -> 0% of each run, Pallas kernels for 6% -> 0%
where the time goes in v1:
time: 279 us; the launch traced here: 275 us
  Pallas kernels  271 us (97%)
    pallas_call x1, Pallas kernels, exchange(): pl.pallas_call(functools.partial(exchange_kernel, count_bits), out_shape=...  171 us
    pallas_call x1, Pallas kernels, forward(): pl.pallas_call(forward_kernel, out_shape=(jax.ShapeDtypeStruct((row_block...  32.2 us
    pallas_call x1, Pallas kernels, inverse(): pl.pallas_call(inverse_kernel, out_shape=jax.ShapeDtypeStruct(matrix.shap...  27.6 us
    pallas_call x1, Pallas kernels, update(): pl.pallas_call(update_kernel, out_shape=jax.ShapeDtypeStruct(cov_tiles.sh...  23.3 us
    pallas_call x1, Pallas kernels, share(): pl.pallas_call(share_kernel, out_shape=jax.ShapeDtypeStruct((many, *packe...  17.7 us

profile of v1, /device:TPU:0, one launch (start us, length us, event | category | flops | bytes accessed | tf_op | source)
XLA Modules:
  0.0 274.6 jit_solution(14454747891406542841)
XLA Ops:
  0.0 0.7 convert_bitcast_fusion
  0.7 0.1 pad.3.clone
  0.7 0.1 copy.6
  0.8 0.7 copy.7
  1.6 1.6 maximum_maximum_fusion.mine_ref
  3.1 17.7 %share.1 = f32[8,32,640]{2,1,0:T(8,128)} custom-call(f32[32,640]{1,0:T(8,128)} %maximum_maximum_fusion.mine_ref), custom_call_target="tpu_custom_call" | custom-call | tf_op jit(solution)/shard_map/share/pallas_call | solution.py:389
  20.8 32.2 %forward.1 = (f32[8,512,256]{2,1,0:T(8,128)}, f32[4,256,512]{2,1,0:T(8,128)}, f32[256,256]{1,0:T(8,128)}) custom-call(s32[32]{0:T(128)} %order_ref.3, f32[256,640]{1,0:T(8,128)} %bitcast.11, f32[4096,2048]{1,0:T(8,128)} %cov_ref.3), custom_call_target="tpu_custom_call" | custom-call | flops 12884901888 | bytes 16777216 | tf_op jit(solution)/shard_map/forward/pallas_call | solution.py:153
  53.0 170.7 %exchange.1 = (f32[2,4,2,256,256]{4,3,2,1,0:T(8,128)}, f32[4,256,512]{2,1,0:T(8,128)}, f32[8,32,256]{2,1,0:T(8,128)}) custom-call(f32[2,4,2,256,256]{4,3,2,1,0:T(8,128)} %bitcast.10, f32[4,256,512]{2,1,0:T(8,128)} %get-tuple-element.12.col_ref, f32[8,32,256]{2,1,0:T(8,128)} %bitcast.12), custom_call_target="tpu_custom_call" | custom-call | tf_op jit(solution)/shard_map/exchange/pallas_call | solution.py:666
  223.7 27.6 %inverse.1.inverse_ref = f32[256,256]{1,0:T(8,128)} custom-call(f32[256,256]{1,0:T(8,128)} %bitcast.15), custom_call_target="tpu_custom_call" | custom-call | flops 400000000 | bytes 524288 | tf_op jit(solution)/shard_map/inverse/pallas_call | solution.py:309
  251.2 23.3 %update.1 = f32[4096,2048]{1,0:T(8,128)} custom-call(s32[32]{0:T(128)} %order_ref.3, f32[8,512,256]{2,1,0:T(8,128)} %bitcast.9, f32[4,256,512]{2,1,0:T(8,128)} %get-tuple-element.15.cols_ref, f32[256,256]{1,0:T(8,128)} %inverse.1.inverse_ref, f32[4096,2048]{1,0:T(8,128)} %cov_ref.3), custom_call_target="tpu_custom_call" | custom-call | flops 6442450944 | bytes 50331648 | tf_op jit(solution)/shard_map/update/pallas_call | solution.py:239
  (1 shorter events, 0.0 us)

commit v2 on v1

--- a/solution.py
+++ b/solution.py
@@ -277,19 +277,22 @@
         work[...] = kept - left * (right * share)
         return carry
 
-    lax.fori_loop(0, size, step, 0)
+    quarter = size // 4
+    for turn in range(4):
+        lax.fori_loop(turn * quarter, (turn + 1) * quarter, step, 0)
+        yield
     return -work[...]
 
 
 def inverse_of(matrix, work):
     size = matrix.shape[0]
     if size <= 128:
-        return swept(matrix, work)
+        return (yield from swept(matrix, work))
     half = size // 2
     upper, corner, lower = matrix[:half, :half], matrix[half:, :half], matrix[half:, half:]
-    upper_inverse = inverse_of(upper, work)
+    upper_inverse = yield from inverse_of(upper, work)
     weight = product(corner, upper_inverse, (1, 0))
-    lower_inverse = inverse_of(lower - product(weight, corner, (1, 1)), work)
+    lower_inverse = yield from inverse_of(lower - product(weight, corner, (1, 1)), work)
     below = -product(lower_inverse, weight, (1, 0))
     above = upper_inverse - product(weight, below, (0, 0))
     return jnp.concatenate(
@@ -297,20 +300,28 @@
     )
 
 
+def inverse_steps(matrix_ref, inverse_ref, work):
+    size = matrix_ref.shape[-1]
+    inverse_ref[...] = yield from inverse_of(matrix_ref[...].reshape(size, size), work)
+
+
 def inverse_kernel(matrix_ref, inverse_ref, work):
-    inverse_ref[...] = inverse_of(matrix_ref[...], work)
+    for _ in inverse_steps(matrix_ref, inverse_ref, work):
+        pass
+
+
+def pivot_size(size):
+    return size if size <= 128 else pivot_size(size // 2)
 
 
 def inverse(matrix):
     size = matrix.shape[0]
-    part = size
-    while part > 128:
-        part //= 2
+    part = pivot_size(size)
     return pl.pallas_call(
         inverse_kernel,
         out_shape=jax.ShapeDtypeStruct(matrix.shape, jnp.float32),
-        in_specs=[pl.BlockSpec(memory_space=pltpu.VMEM)],
-        out_specs=pl.BlockSpec(memory_space=pltpu.VMEM),
+        in_specs=[VMEM],
+        out_specs=VMEM,
         scratch_shapes=[pltpu.VMEM((part, part), jnp.float32)],
         cost_estimate=pl.CostEstimate(flops=400_000_000, bytes_accessed=8 * size * size, transcendentals=0),
         name="inverse",
@@ -349,7 +360,7 @@
     return (
         cross_rows.reshape(row_blocks, size, count_obs),
         cross_cols.reshape(col_blocks, size, count_obs).transpose(0, 2, 1),
-        innovation,
+        inverse(innovation),
     )
 
 
@@ -362,26 +373,37 @@
         return self.count - number
 
 
-def share_kernel(mine_ref, all_ref, send, recv):
+def share_kernel(mine_ref, all_ref, send, recv, core_send, core_recv):
     row, col = lax.axis_index("tr"), lax.axis_index("tc")
-    many = all_ref.shape[0]
-    copies = [
-        pltpu.make_async_remote_copy(
-            mine_ref, all_ref.at[col], send.at[step], recv.at[step],
-            device_id=(row, lax.rem(col + step, many)), device_id_type=pl.DeviceIdType.MESH,
+    chips = all_ref.shape[0] // 2
+    chip, core = col // 2, col % 2
+
+    def copy(source, block, step):
+        return pltpu.make_async_remote_copy(
+            source, all_ref.at[block], send.at[step], recv.at[step],
+            device_id=(row, 2 * lax.rem(chip + step, chips) + core), device_id_type=pl.DeviceIdType.MESH,
         )
-        for step in range(1, many)
-    ]
-    for copy in copies:
-        copy.start()
+
+    def beside(source, block, step):
+        return pltpu.make_async_remote_copy(
+            source, all_ref.at[block], core_send.at[step], core_recv.at[step],
+            device_id=(row, 2 * chip + 1 - core), device_id_type=pl.DeviceIdType.MESH,
+        )
+
+    sent = [copy(mine_ref, col, step) for step in range(1, chips)]
+    sent.append(beside(mine_ref, col, 0))
+    for one in sent:
+        one.start()
     all_ref[col] = mine_ref[...]
-    for copy in copies:
-        copy.wait_send()
-    for step in range(1, many):
-        pltpu.make_async_remote_copy(
-            mine_ref, all_ref.at[lax.rem(col + many - step, many)], send.at[step], recv.at[step],
-            device_id=(row, lax.rem(col + step, many)), device_id_type=pl.DeviceIdType.MESH,
-        ).wait_recv()
+    for step in range(1, chips):
+        block = 2 * lax.rem(chip + chips - step, chips) + core
+        copy(mine_ref, block, step).wait_recv()
+        sent.append(beside(all_ref.at[block], block, step))
+        sent[-1].start()
+    for step in range(chips):
+        beside(mine_ref, 2 * lax.rem(chip + chips - step, chips) + 1 - core, step).wait_recv()
+    for one in sent:
+        one.wait_send()
 
 
 def share(packed):
@@ -391,7 +413,7 @@
         out_shape=jax.ShapeDtypeStruct((many, *packed.shape), f32),
         in_specs=[VMEM],
         out_specs=VMEM,
-        scratch_shapes=[pltpu.SemaphoreType.DMA((many,)), pltpu.SemaphoreType.DMA((many,))],
+        scratch_shapes=[pltpu.SemaphoreType.DMA((many // 2,))] * 4,
         compiler_params=pltpu.CompilerParams(has_side_effects=True),
         name="share",
     )(packed)
@@ -399,8 +421,8 @@
 
 
 def exchange_kernel(
-    count_bits, row_ref, col_ref, gram_ref, rows_out, cols_out, gram_out,
-    send, recv, from_core, sums, landed, upward, downward, rows_here, cols_here, total,
+    count_bits, row_ref, col_ref, gram_ref, rows_out, cols_out, inverse_out,
+    gram_out, work, send, recv, from_core, sums, landed, upward, downward, rows_here, cols_here, total,
     gram_work, gram_core, gram_bits, gram_line,
 ):
     sems = Sems()
@@ -442,16 +464,16 @@
         def _():
             copy(col_ref.at[other], downward.at[other], down + other, (z - 1, j)).start()
 
-    def line_pass(step):
-        chunk, other = line - step, step - 1
-
-        @pl.when((z > 0) & (z < chunk))
+    def line_round(step):
+        chunk, other = z + line - 1 - step, z - line + 1 + step
+
+        @pl.when((z > 0) & (chunk < line))
         def _():
             copy(upward.at[chunk], upward.at[chunk], up + chunk).wait_recv()
             upward[chunk] += col_ref[chunk]
             copy(upward.at[chunk], upward.at[chunk], up + chunk, (z + 1, j)).start()
 
-        @pl.when((z < line - 1) & (z > other))
+        @pl.when((z < line - 1) & (other >= 0))
         def _():
             copy(downward.at[other], downward.at[other], down + other).wait_recv()
             downward[other] += col_ref[other]
@@ -543,22 +565,41 @@
     core_sum.wait_recv()
     sums[...] = row_ref[core] + from_core[...]
     made = plane_send(0)
-    for step in range(1, line):
-        copy(gram_work.at[mine], gram_line.at[lax.rem(z + line - step, line)], base + step).wait()
-    gram_out[mine] = sum(gram_line[step] for step in range(line))
-    line_pass(1)
-    for number in range(count_bits):
-        size = 2**number
-        start = core * held + chip // size * size
-        begin(gram_out.at[pl.ds(start, size)], gram_out.at[pl.ds(start, size)], across(number)).wait_recv()
-    begin(gram_out.at[pl.ds(core * held, held)], gram_out.at[pl.ds(core * held, held)], beside).wait_recv()
-    for step in range(1, max(line - 1, count_bits)):
+
+    def gram_back():
+        for step in range(1, line):
+            copy(gram_work.at[mine], gram_line.at[lax.rem(z + line - step, line)], base + step).wait()
+        gram_out[mine] = sum(gram_line[step] for step in range(line))
+        for number in range(count_bits):
+            size = 2**number
+            spot = gram_out.at[pl.ds(core * held + chip // size * size, size)]
+            sent = begin(spot, spot, across(number))
+            yield
+            sent.wait_recv()
+        spot = gram_out.at[pl.ds(core * held, held)]
+        sent = begin(spot, spot, beside)
+        yield
+        sent.wait_recv()
+
+    gram_turns = gram_back()
+    for step in range(1, line - 1):
+        line_round(step)
+        next(gram_turns, None)
         if step < count_bits:
             plane_add(step - 1, made)
             made = plane_send(step)
-        if step + 1 < line - 1:
-            line_pass(step + 1)
+            next(gram_turns, None)
+    for _ in gram_turns:
+        pass
+    for step in range(max(line - 1, 1), count_bits):
+        plane_add(step - 1, made)
+        made = plane_send(step)
     plane_add(count_bits - 1, made)
+    inverse_turns = inverse_steps(gram_out, inverse_out, work)
+
+    def fill(number):
+        for _ in range(number):
+            next(inverse_turns, None)
 
     to_rows, to_cols = sems.take(), sems.take()
     partner = (chip, 2 * z + core)
@@ -568,8 +609,7 @@
     def _():
         copy(sums.at[chip], rows_here, to_rows, partner).start()
 
-    if line > 2:
-        line_pass(line - 1)
+    fill(1)
     line_end()
 
     @pl.when(apart)
@@ -621,6 +661,7 @@
                 copy(cols_out.at[other], cols_out.at[other], back + other).wait_send()
 
     line_spread(1)
+    fill(2)
 
     @pl.when(apart)
     def _():
@@ -629,22 +670,29 @@
     for part in range(parts):
         lanes = slice(part * width, (part + 1) * width)
         rows_out[core, chip, part] = sums[chip, part] + cols_here[:, lanes].T
+
+    def plane_spread(turn):
+        if turn == count_bits:
+            return [begin(rows_out.at[core], rows_out.at[core], beside)]
+        made = []
+        for part in range(parts):
+            number, picks = chosen(part, count_bits - 1 - turn, False)
+            for pick in picks:
+                spot = rows_out.at[core, pick, part]
+                made.append(begin(spot, spot, across(number)))
+        return made
 
     made = []
     for turn in range(max(line, count_bits + 1)):
         for one in made:
             one.wait_recv()
-        made = []
+        made = plane_spread(turn) if turn <= count_bits else []
+        if turn == count_bits:
+            fill(64)
+        if turn + 2 <= line:
+            line_spread(turn + 2)
         if turn < count_bits:
-            for part in range(parts):
-                number, picks = chosen(part, count_bits - 1 - turn, False)
-                for pick in picks:
-                    spot = rows_out.at[core, pick, part]
-                    made.append(begin(spot, spot, across(number)))
-        elif turn == count_bits:
-            made = [begin(rows_out.at[core], rows_out.at[core], beside)]
-        if 1 <= turn < line:
-            line_spread(turn + 1)
+            fill(2)
     for one in made:
         one.wait_recv()
     line_spread_sent()
@@ -663,12 +711,15 @@
     cols = col_part.shape
     gram = (many, seg, count_obs)
     landings = sum(parts * 2 ** (count_bits - 1 - step) for step in range(count_bits))
-    cross_rows, cross_cols, innovation = pl.pallas_call(
+    part = pivot_size(count_obs)
+    cross_rows, cross_cols, inverted = pl.pallas_call(
         functools.partial(exchange_kernel, count_bits),
-        out_shape=tuple(jax.ShapeDtypeStruct(shape, f32) for shape in (rows, cols, gram)),
+        out_shape=tuple(jax.ShapeDtypeStruct(shape, f32) for shape in (rows, cols, gram_part.shape)),
         in_specs=[VMEM] * 3,
         out_specs=(VMEM,) * 3,
         scratch_shapes=[
+            pltpu.VMEM(gram, f32),
+            pltpu.VMEM((part, part), f32),
             pltpu.SemaphoreType.DMA((96,)),
             pltpu.SemaphoreType.DMA((96,)),
             pltpu.VMEM(rows[1:], f32),
@@ -687,7 +738,7 @@
         compiler_params=pltpu.CompilerParams(has_side_effects=True),
         name="exchange",
     )(row_part.reshape(rows), col_part, gram_part.reshape(gram))
-    return cross_rows.reshape(row_part.shape), cross_cols, innovation.reshape(gram_part.shape)
+    return cross_rows.reshape(row_part.shape), cross_cols, inverted
 
 
 def body(cov_tiles, block_order, stations, obs_values, obs_error):
@@ -698,8 +749,8 @@
     square = many == 2 * line and line & (line - 1) == 0 and line > 1
     whole_tiles = row_part.shape[0] == many and col_part.shape[0] == line
     spread = exchange if square and whole_tiles else exchange_plain
-    cross_rows, cross_cols, innovation = spread(row_part, col_part, gram_part)
-    return update(block_order, cross_rows, cross_cols, inverse(innovation), cov_tiles)
+    cross_rows, cross_cols, inverted = spread(row_part, col_part, gram_part)
+    return update(block_order, cross_rows, cross_cols, inverted, cov_tiles)
 
 
 def solution(mesh):

time: 279 us -> 238 us (0.85)
  Pallas kernels: 271 us -> 232 us
    pallas_call x1 -> x0, Pallas kernels: 27.6 us -> none  [inverse(): pl.pallas_call(inverse_kernel, out_shape=jax.ShapeDtypeStruct(matrix.shap...]
    pallas_call x1, Pallas kernels: 32.2 us -> 23.9 us  [forward(): pl.pallas_call(forward_kernel, out_shape=(jax.ShapeDtypeStruct((row_block...]
where the time goes in v2:
time: 238 us; the launch traced here: 235 us
  Pallas kernels  232 us (97%)
    pallas_call x1, Pallas kernels, exchange(): pl.pallas_call(functools.partial(exchange_kernel, count_bits), out_shape=...  170 us
    pallas_call x1, Pallas kernels, forward(): pl.pallas_call(forward_kernel, out_shape=(jax.ShapeDtypeStruct((row_block...  23.9 us
    pallas_call x1, Pallas kernels, update(): pl.pallas_call(update_kernel, out_shape=jax.ShapeDtypeStruct(cov_tiles.sh...  21.2 us
    pallas_call x1, Pallas kernels, share(): pl.pallas_call(share_kernel, out_shape=jax.ShapeDtypeStruct((many, *packe...  16.4 us

profile of v2, /device:TPU:0, one launch (start us, length us, event | category | flops | bytes accessed | tf_op | source)
XLA Modules:
  0.0 235.0 jit_solution(8155614586730132703)
XLA Ops:
  0.0 0.7 convert_bitcast_fusion
  0.7 0.1 pad.3.clone
  0.7 0.1 copy.6
  0.8 0.7 copy.7
  1.6 1.6 maximum_maximum_fusion.mine_ref
  3.1 16.4 %share.1 = f32[8,32,640]{2,1,0:T(8,128)} custom-call(f32[32,640]{1,0:T(8,128)} %maximum_maximum_fusion.mine_ref), custom_call_target="tpu_custom_call" | custom-call | tf_op jit(solution)/shard_map/share/pallas_call | solution.py:411
  19.5 23.9 %forward.1 = (f32[8,512,256]{2,1,0:T(8,128)}, f32[4,256,512]{2,1,0:T(8,128)}, f32[256,256]{1,0:T(8,128)}) custom-call(s32[32]{0:T(128)} %order_ref.3, f32[256,640]{1,0:T(8,128)} %bitcast.10, f32[4096,2048]{1,0:T(8,128)} %cov_ref.3), custom_call_target="tpu_custom_call" | custom-call | flops 12884901888 | bytes 16777216 | tf_op jit(solution)/shard_map/forward/pallas_call | solution.py:153
  43.4 170.4 %exchange.1 = (f32[2,4,2,256,256]{4,3,2,1,0:T(8,128)}, f32[4,256,512]{2,1,0:T(8,128)}, f32[256,256]{1,0:T(8,128)}) custom-call(f32[2,4,2,256,256]{4,3,2,1,0:T(8,128)} %bitcast.9, f32[4,256,512]{2,1,0:T(8,128)} %get-tuple-element.12.col_ref, f32[8,32,256]{2,1,0:T(8,128)} %bitcast.11), custom_call_target="tpu_custom_call" | custom-call | tf_op jit(solution)/shard_map/exchange/pallas_call | solution.py:715
  213.8 21.2 %update.1 = f32[4096,2048]{1,0:T(8,128)} custom-call(s32[32]{0:T(128)} %order_ref.3, f32[8,512,256]{2,1,0:T(8,128)} %bitcast.8, f32[4,256,512]{2,1,0:T(8,128)} %get-tuple-element.15.cols_ref, f32[256,256]{1,0:T(8,128)} %get-tuple-element.16.inverse_ref, f32[4096,2048]{1,0:T(8,128)} %cov_ref.3), custom_call_target="tpu_custom_call" | custom-call | flops 6442450944 | bytes 50331648 | tf_op jit(solution)/shard_map/update/pallas_call | solution.py:239
  (1 shorter events, 0.0 us)

commit v3 on v2

--- a/solution.py
+++ b/solution.py
@@ -422,7 +422,7 @@
 
 def exchange_kernel(
     count_bits, row_ref, col_ref, gram_ref, rows_out, cols_out, inverse_out,
-    gram_out, work, send, recv, from_core, sums, landed, upward, downward, rows_here, cols_here, total,
+    gram_out, work, send, recv, from_core, sums, landed, upward, downward, rows_here, cols_here, total, relay,
     gram_work, gram_core, gram_bits, gram_line,
 ):
     sems = Sems()
@@ -450,6 +450,18 @@
 
     def across(number):
         return z, 2 * (chip + (1 - 2 * bit(number)) * 2**number) + core
+
+    def mixed(value, plane):
+        return sum(
+            (value // 2**number + plane // 2 ** (count_bits - 1 - number)) % 2 * 2**number
+            for number in range(count_bits)
+        )
+
+    def plane_of(value, chunk):
+        return sum(
+            (value // 2**number + chunk // 2**number) % 2 * 2 ** (count_bits - 1 - number)
+            for number in range(count_bits)
+        )
 
     up, down = sems.take(line), sems.take(line)
 
@@ -563,7 +575,9 @@
         line_begin(step)
 
     core_sum.wait_recv()
-    sums[...] = row_ref[core] + from_core[...]
+    for owner in range(line):
+        chunk = mixed(owner, z)
+        sums[owner] = row_ref[core, chunk] + from_core[chunk]
     made = plane_send(0)
 
     def gram_back():
@@ -601,26 +615,46 @@
         for _ in range(number):
             next(inverse_turns, None)
 
-    to_rows, to_cols = sems.take(), sems.take()
-    partner = (chip, 2 * z + core)
-    apart = z != chip
+    to_cols, first_leg, second_leg = sems.take(), sems.take(2), sems.take(2)
+    owned = mixed(chip, z)
+    apart = (owned != z) | (z != chip)
+    column = (owned, 2 * z + core)
+    via = mixed(z, chip)
+    beyond = plane_of(chip, z)
 
     @pl.when(apart)
     def _():
-        copy(sums.at[chip], rows_here, to_rows, partner).start()
-
-    fill(1)
-    line_end()
-
-    @pl.when(apart)
-    def _():
-        copy(total, cols_here, to_cols, partner).start()
-        copy(sums.at[chip], rows_here, to_rows, partner).wait()
+        copy(sums.at[chip], rows_here, to_cols, column).start()
 
     @pl.when(jnp.logical_not(apart))
     def _():
         rows_here[...] = sums[chip]
-        cols_here[...] = total[...]
+
+    fill(1)
+    line_end()
+
+    def piece(ref, number):
+        size = total.shape[0] // 2
+        return ref.at[pl.ds(number * size, size)]
+
+    def leg_one(number):
+        return copy(piece(total, number), piece(relay, number), first_leg + number, (z, 2 * via + core))
+
+    def leg_two(number):
+        return copy(piece(relay, number), piece(cols_here, number), second_leg + number, (beyond, j))
+
+    @pl.when(via != chip)
+    def _():
+        leg_one(0).start()
+        leg_one(1).start()
+
+    @pl.when(via == chip)
+    def _():
+        relay[...] = total[...]
+
+    @pl.when(apart)
+    def _():
+        copy(sums.at[chip], rows_here, to_cols, column).wait()
 
     for part in range(parts):
         lanes = slice(part * width, (part + 1) * width)
@@ -661,39 +695,52 @@
                 copy(cols_out.at[other], cols_out.at[other], back + other).wait_send()
 
     line_spread(1)
-    fill(2)
-
-    @pl.when(apart)
+    for number in range(2):
+
+        @pl.when(via != chip)
+        def _():
+            leg_one(number).wait()
+
+        @pl.when(beyond != z)
+        def _():
+            leg_two(number).start()
+
+    @pl.when(beyond == z)
     def _():
-        copy(total, cols_here, to_cols, partner).wait()
+        cols_here[...] = relay[...]
+
+    fill(3)
+
+    @pl.when(beyond != z)
+    def _():
+        leg_two(0).wait()
+        leg_two(1).wait()
 
     for part in range(parts):
         lanes = slice(part * width, (part + 1) * width)
-        rows_out[core, chip, part] = sums[chip, part] + cols_here[:, lanes].T
-
-    def plane_spread(turn):
-        if turn == count_bits:
-            return [begin(rows_out.at[core], rows_out.at[core], beside)]
-        made = []
+        rows_out[core, owned, part] = sums[chip, part] + cols_here[:, lanes].T
+
+    def spots(turn, flip):
         for part in range(parts):
-            number, picks = chosen(part, count_bits - 1 - turn, False)
+            number, picks = chosen(part, count_bits - 1 - turn, flip)
             for pick in picks:
-                spot = rows_out.at[core, pick, part]
-                made.append(begin(spot, spot, across(number)))
-        return made
-
-    made = []
-    for turn in range(max(line, count_bits + 1)):
-        for one in made:
-            one.wait_recv()
-        made = plane_spread(turn) if turn <= count_bits else []
+                yield number, rows_out.at[core, mixed(pick, z), part]
+
+    beside_copies = [begin(rows_out.at[core, owned], rows_out.at[core, owned], beside)]
+    for turn in range(max(line - 1, count_bits)):
+        if turn < count_bits:
+            made = [begin(spot, spot, across(number)) for number, spot in spots(turn, False)]
         if turn == count_bits:
             fill(64)
         if turn + 2 <= line:
             line_spread(turn + 2)
         if turn < count_bits:
             fill(2)
-    for one in made:
+            for one in made:
+                one.wait_recv()
+            beside_copies += [begin(spot, spot, beside) for _, spot in spots(turn, True)]
+    fill(64)
+    for one in beside_copies:
         one.wait_recv()
     line_spread_sent()
     line_sent()
@@ -730,6 +777,7 @@
             pltpu.VMEM(rows[2:], f32),
             pltpu.VMEM(cols[1:], f32),
             pltpu.VMEM(cols[1:], f32),
+            pltpu.VMEM(cols[1:], f32),
             pltpu.VMEM(gram, f32),
             pltpu.VMEM((many // 2, seg, count_obs), f32),
             pltpu.VMEM((many // 2, seg, count_obs), f32),

time: 238 us -> 191 us (0.80); the launches traced: 235 us -> 193 us
  Pallas kernels: 232 us -> 190 us
    pallas_call x1, Pallas kernels: 170 us -> 115 us  [exchange(): pl.pallas_call(functools.partial(exchange_kernel, count_bits), out_shape=...]
    pallas_call x1, Pallas kernels: 23.9 us -> 34.5 us  [forward(): pl.pallas_call(forward_kernel, out_shape=(jax.ShapeDtypeStruct((row_block...]
    pallas_call x1, Pallas kernels: 21.2 us -> 23.8 us  [update(): pl.pallas_call(update_kernel, out_shape=jax.ShapeDtypeStruct(cov_tiles.sh...]
where the time goes in v3:
time: 191 us; the launch traced here: 193 us
  Pallas kernels  190 us (99%)
  other arithmetic  2.21 us (1%)
    pallas_call x1, Pallas kernels, exchange(): pl.pallas_call(functools.partial(exchange_kernel, count_bits), out_shape=...  115 us
    pallas_call x1, Pallas kernels, forward(): pl.pallas_call(forward_kernel, out_shape=(jax.ShapeDtypeStruct((row_block...  34.5 us
    pallas_call x1, Pallas kernels, update(): pl.pallas_call(update_kernel, out_shape=jax.ShapeDtypeStruct(cov_tiles.sh...  23.8 us
    pallas_call x1, Pallas kernels, share(): pl.pallas_call(share_kernel, out_shape=jax.ShapeDtypeStruct((many, *packe...  16.4 us

profile of v3, /device:TPU:0, one launch (start us, length us, event | category | flops | bytes accessed | tf_op | source)
XLA Modules:
  0.0 193.0 jit_solution(10028716180329880463)
XLA Ops:
  0.0 0.7 convert_bitcast_fusion
  0.7 0.1 pad.3.clone
  0.7 0.1 copy.6
  0.8 0.7 copy.7
  1.6 1.6 maximum_maximum_fusion.mine_ref
  3.1 16.4 %share.1 = f32[8,32,640]{2,1,0:T(8,128)} custom-call(f32[32,640]{1,0:T(8,128)} %maximum_maximum_fusion.mine_ref), custom_call_target="tpu_custom_call" | custom-call | tf_op jit(solution)/shard_map/share/pallas_call | solution.py:411
  19.5 34.5 %forward.1 = (f32[8,512,256]{2,1,0:T(8,128)}, f32[4,256,512]{2,1,0:T(8,128)}, f32[256,256]{1,0:T(8,128)}) custom-call(s32[32]{0:T(128)} %order_ref.3, f32[256,640]{1,0:T(8,128)} %bitcast.10, f32[4096,2048]{1,0:T(8,128)} %cov_ref.3), custom_call_target="tpu_custom_call" | custom-call | flops 12884901888 | bytes 16777216 | tf_op jit(solution)/shard_map/forward/pallas_call | solution.py:153
  54.0 115.1 %exchange.1 = (f32[2,4,2,256,256]{4,3,2,1,0:T(8,128)}, f32[4,256,512]{2,1,0:T(8,128)}, f32[256,256]{1,0:T(8,128)}) custom-call(f32[2,4,2,256,256]{4,3,2,1,0:T(8,128)} %bitcast.9, f32[4,256,512]{2,1,0:T(8,128)} %get-tuple-element.12.col_ref, f32[8,32,256]{2,1,0:T(8,128)} %bitcast.11), custom_call_target="tpu_custom_call" | custom-call | tf_op jit(solution)/shard_map/exchange/pallas_call | solution.py:762
  169.1 23.8 %update.1 = f32[4096,2048]{1,0:T(8,128)} custom-call(s32[32]{0:T(128)} %order_ref.3, f32[8,512,256]{2,1,0:T(8,128)} %bitcast.8, f32[4,256,512]{2,1,0:T(8,128)} %get-tuple-element.15.cols_ref, f32[256,256]{1,0:T(8,128)} %get-tuple-element.16.inverse_ref, f32[4096,2048]{1,0:T(8,128)} %cov_ref.3), custom_call_target="tpu_custom_call" | custom-call | flops 6442450944 | bytes 50331648 | tf_op jit(solution)/shard_map/update/pallas_call | solution.py:239
  (1 shorter events, 0.0 us)

commit v4 on v3

--- a/solution.py
+++ b/solution.py
@@ -69,12 +69,24 @@
     ]
 
 
+def sorted_by_station(packed, size):
+    count = packed.shape[0]
+    codes = packed[:, size:size + 1]
+    codes_across = packed[:, size:].T[0:1, :]
+    down = lax.broadcasted_iota(i32, (count, count), 0)
+    across = lax.broadcasted_iota(i32, (count, count), 1)
+    earlier = (codes < codes_across) | ((codes == codes_across) & (down < across))
+    rank = jnp.sum(jnp.where(earlier, 1.0, 0.0), axis=0, keepdims=True).astype(i32)
+    return product(jnp.where(down == rank, 1.0, 0.0), packed, (1, 0))
+
+
 def forward_kernel(
     order_ref, packed_ref, cov_ref, rows_ref, cols_ref, gram_ref,
-    live_ref, held, sem, for_rows, for_cols,
+    live_ref, used_rows, used_cols, held, sem, for_rows, for_cols,
 ):
     row_blocks, size, count_obs = rows_ref.shape
     col_blocks = cols_ref.shape[0]
+    windows, span = for_rows.shape[1], for_rows.shape[2] // 2
     row_first = lax.axis_index("tr") * row_blocks
     col_first = lax.axis_index("tc") * col_blocks
     count = list_tiles(order_ref, live_ref, row_blocks, col_blocks)
@@ -91,21 +103,38 @@
         def _():
             fetch(at).start()
 
-    values = packed_ref[:, :size]
-    extras = packed_ref[:, size:]
+    packed = sorted_by_station(packed_ref[...], size)
+    values = packed[:, :size]
+    extras = packed[:, size:]
     codes_down = extras[:, 0:1].astype(i32)
     flipped = extras.T
     codes_across = flipped[0:1, :].astype(i32)
     errors_across = flipped[1:2, :]
     values_t = values.T
-    for block in range(row_blocks):
-        chosen = jnp.where(codes_down == order_ref[row_first + block], values, 0.0)
-        for_rows[block, 0], for_rows[block, 1] = halves(chosen)
-    for block in range(col_blocks):
-        chosen = jnp.where(codes_across == order_ref[col_first + block], values_t, 0.0)
-        for_cols[block, 0], for_cols[block, 1] = halves(chosen)
+    for window in range(windows):
+        here = slice(window * span, (window + 1) * span)
+        for block in range(row_blocks):
+            match = codes_down[here] == order_ref[row_first + block]
+            high, low = halves(jnp.where(match, values[here], 0.0))
+            for_rows[block, window] = jnp.concatenate((high, low), axis=0)
+            same = codes_across[:, here] == order_ref[row_first + block]
+            used_rows[block * windows + window] = jnp.sum(jnp.where(same, 1, 0))
+        for block in range(col_blocks):
+            match = codes_across[:, here] == order_ref[col_first + block]
+            high, low = halves(jnp.where(match, values_t[:, here], 0.0))
+            for_cols[block, window] = jnp.concatenate((high, low), axis=1)
+            used_cols[block * windows + window] = jnp.sum(jnp.where(match, 1, 0))
     rows_ref[...] = jnp.zeros_like(rows_ref)
     cols_ref[...] = jnp.zeros_like(cols_ref)
+    gram_ref[...] = jnp.zeros_like(gram_ref)
+
+    def times_cols(parts, block, window):
+        both = dot(parts[0], for_cols[block, window]) + dot(parts[1], for_cols[block, window])
+        return both[:, :span] + both[:, span:]
+
+    def rows_times(parts, block, window):
+        both = dot(for_rows[block, window], parts[0])
+        return both[:span] + both[span:] + dot(for_rows[block, window, :span], parts[1])
 
     def step(at, carry):
         tile = live_ref[at]
@@ -117,30 +146,46 @@
             fetch(at + DEPTH - 1).start()
 
         fetch(at).wait()
-        parts = halves(held[slot])
-        rows_ref[row] += dot3(parts, (for_cols[col, 0], for_cols[col, 1]))
-
-        @pl.when(row_first + row != col_first + col)
-        def _():
-            cols_ref[col] += dot3((for_rows[row, 0], for_rows[row, 1]), parts)
+        strict = row_first + row != col_first + col
+        for window in range(windows):
+            here = slice(window * span, (window + 1) * span)
+
+            @pl.when(used_cols[col * windows + window] > 0)
+            def _():
+                rows_ref[row, :, here] += times_cols(halves(held[slot]), col, window)
+
+            @pl.when(strict & (used_rows[row * windows + window] > 0))
+            def _():
+                cols_ref[col, here] += rows_times(halves(held[slot]), row, window)
 
         return carry
 
     lax.fori_loop(0, count, step, 0)
+
+    def add_col(block, carry):
+        for window in range(windows):
+            here = slice(window * span, (window + 1) * span)
+
+            @pl.when(used_cols[block * windows + window] > 0)
+            def _():
+                gram_ref[:, here] += times_cols(halves(cols_ref[block]), block, window)
+
+        return carry
+
+    lax.fori_loop(0, col_blocks, add_col, 0)
     first = (lax.axis_index("tr") == 0) & (lax.axis_index("tc") == 0)
     across = lax.broadcasted_iota(i32, (count_obs, count_obs), 1)
     down = lax.broadcasted_iota(i32, (count_obs, count_obs), 0)
-    gram_ref[...] = jnp.zeros_like(gram_ref)
-
-    def add_col(block, carry):
-        gram_ref[...] += dot3(halves(cols_ref[block]), (for_cols[block, 0], for_cols[block, 1]))
-        return carry
-
-    lax.fori_loop(0, col_blocks, add_col, 0)
     gram_ref[...] = gram_ref[...].T + jnp.where((across == down) & first, errors_across, 0.0)
 
     def add_row(block, carry):
-        gram_ref[...] += dot3((for_rows[block, 0], for_rows[block, 1]), halves(rows_ref[block]))
+        for window in range(windows):
+            here = slice(window * span, (window + 1) * span)
+
+            @pl.when(used_rows[block * windows + window] > 0)
+            def _():
+                gram_ref[here] += rows_times(halves(rows_ref[block]), block, window)
+
         return carry
 
     lax.fori_loop(0, row_blocks, add_row, 0)
@@ -150,6 +195,8 @@
     count_obs = packed.shape[0]
     row_blocks, col_blocks = cov_tiles.shape[0] // size, cov_tiles.shape[1] // size
     tiles = row_blocks * col_blocks
+    span = pivot_size(count_obs)
+    windows = count_obs // span
     return pl.pallas_call(
         forward_kernel,
         out_shape=(
@@ -161,10 +208,12 @@
         out_specs=(VMEM, VMEM, VMEM),
         scratch_shapes=[
             pltpu.SMEM((tiles,), i32),
+            pltpu.SMEM((row_blocks * windows,), i32),
+            pltpu.SMEM((col_blocks * windows,), i32),
             pltpu.VMEM((DEPTH, size, size), f32),
             pltpu.SemaphoreType.DMA((DEPTH,)),
-            pltpu.VMEM((row_blocks, 2, count_obs, size), bf16),
-            pltpu.VMEM((col_blocks, 2, size, count_obs), bf16),
+            pltpu.VMEM((row_blocks, windows, 2 * span, size), bf16),
+            pltpu.VMEM((col_blocks, windows, size, 2 * span), bf16),
         ],
         cost_estimate=pl.CostEstimate(
             flops=6 * tiles * size * size * count_obs, bytes_accessed=2 * tiles * size * size, transcendentals=0

time: 191 us -> 188 us (0.984); the launches traced: 193 us -> 188 us
  Pallas kernels: 190 us -> 184 us
    pallas_call x1, Pallas kernels: 34.5 us -> 29.6 us  [forward(): pl.pallas_call(forward_kernel, out_shape=(jax.ShapeDtypeStruct((row_block...]
where the time goes in v4:
time: 188 us
  Pallas kernels  184 us (98%)
  other arithmetic  2.21 us (1%)
    pallas_call x1, Pallas kernels, exchange(): pl.pallas_call(functools.partial(exchange_kernel, count_bits), out_shape=...  115 us
    pallas_call x1, Pallas kernels, forward(): pl.pallas_call(forward_kernel, out_shape=(jax.ShapeDtypeStruct((row_block...  29.6 us
    pallas_call x1, Pallas kernels, update(): pl.pallas_call(update_kernel, out_shape=jax.ShapeDtypeStruct(cov_tiles.sh...  23.9 us
    pallas_call x1, Pallas kernels, share(): pl.pallas_call(share_kernel, out_shape=jax.ShapeDtypeStruct((many, *packe...  16.4 us

profile of v4, /device:TPU:0, one launch (start us, length us, event | category | flops | bytes accessed | tf_op | source)
XLA Modules:
  0.0 187.6 jit_solution(10953700014750077060)
XLA Ops:
  0.0 0.7 convert_bitcast_fusion
  0.7 0.1 pad.3.clone
  0.7 0.1 copy.6
  0.8 0.7 copy.7
  1.6 1.6 maximum_maximum_fusion.mine_ref
  3.1 16.4 %share.1 = f32[8,32,640]{2,1,0:T(8,128)} custom-call(f32[32,640]{1,0:T(8,128)} %maximum_maximum_fusion.mine_ref), custom_call_target="tpu_custom_call" | custom-call | tf_op jit(solution)/shard_map/share/pallas_call | solution.py:460
  19.5 29.6 %forward.1 = (f32[8,512,256]{2,1,0:T(8,128)}, f32[4,256,512]{2,1,0:T(8,128)}, f32[256,256]{1,0:T(8,128)}) custom-call(s32[32]{0:T(128)} %order_ref.3, f32[256,640]{1,0:T(8,128)} %bitcast.10, f32[4096,2048]{1,0:T(8,128)} %cov_ref.3), custom_call_target="tpu_custom_call" | custom-call | flops 12884901888 | bytes 16777216 | tf_op jit(solution)/shard_map/forward/pallas_call | solution.py:200
  49.1 114.6 %exchange.1 = (f32[2,4,2,256,256]{4,3,2,1,0:T(8,128)}, f32[4,256,512]{2,1,0:T(8,128)}, f32[256,256]{1,0:T(8,128)}) custom-call(f32[2,4,2,256,256]{4,3,2,1,0:T(8,128)} %bitcast.9, f32[4,256,512]{2,1,0:T(8,128)} %get-tuple-element.12.col_ref, f32[8,32,256]{2,1,0:T(8,128)} %bitcast.11), custom_call_target="tpu_custom_call" | custom-call | tf_op jit(solution)/shard_map/exchange/pallas_call | solution.py:811
  163.7 23.9 %update.1 = f32[4096,2048]{1,0:T(8,128)} custom-call(s32[32]{0:T(128)} %order_ref.3, f32[8,512,256]{2,1,0:T(8,128)} %bitcast.8, f32[4,256,512]{2,1,0:T(8,128)} %get-tuple-element.15.cols_ref, f32[256,256]{1,0:T(8,128)} %get-tuple-element.16.inverse_ref, f32[4096,2048]{1,0:T(8,128)} %cov_ref.3), custom_call_target="tpu_custom_call" | custom-call | flops 6442450944 | bytes 50331648 | tf_op jit(solution)/shard_map/update/pallas_call | solution.py:288
  (1 shorter events, 0.0 us)

commit v5 on v4

--- a/solution.py
+++ b/solution.py
@@ -69,19 +69,24 @@
     ]
 
 
-def sorted_by_station(packed, size):
+def sorted_by_position(packed, size, order_ref):
     count = packed.shape[0]
-    codes = packed[:, size:size + 1]
-    codes_across = packed[:, size:].T[0:1, :]
+    codes = packed[:, size:].T[0:1, :].astype(i32)
+    places_across = sum(jnp.where(codes == order_ref[place], place, 0) for place in range(order_ref.shape[0]))
+    places = jnp.broadcast_to(places_across.astype(f32), (128, count)).T[:, 0:1].astype(i32)
     down = lax.broadcasted_iota(i32, (count, count), 0)
     across = lax.broadcasted_iota(i32, (count, count), 1)
-    earlier = (codes < codes_across) | ((codes == codes_across) & (down < across))
+    earlier = (places < places_across) | ((places == places_across) & (down < across))
     rank = jnp.sum(jnp.where(earlier, 1.0, 0.0), axis=0, keepdims=True).astype(i32)
-    return product(jnp.where(down == rank, 1.0, 0.0), packed, (1, 0))
+    return product(jnp.where(down == rank, 1.0, 0.0), packed, (1, 0)), places_across
+
+
+def reach(count, groups):
+    return tuple(min(count, (count * (group + 1) // groups + count // 8 + 7) // 8 * 8) for group in range(groups))
 
 
 def forward_kernel(
-    order_ref, packed_ref, cov_ref, rows_ref, cols_ref, gram_ref,
+    order_ref, packed_ref, cov_ref, rows_ref, cols_ref, gram_ref, fits_ref,
     live_ref, used_rows, used_cols, held, sem, for_rows, for_cols,
 ):
     row_blocks, size, count_obs = rows_ref.shape
@@ -103,7 +108,14 @@
         def _():
             fetch(at).start()
 
-    packed = sorted_by_station(packed_ref[...], size)
+    packed, places = sorted_by_position(packed_ref[...], size, order_ref)
+    groups = lax.axis_size("tr")
+    limits = reach(count_obs, groups)
+    fits = jnp.int32(1)
+    for group in range(groups - 1):
+        before = jnp.sum(jnp.where(places < (group + 1) * row_blocks, 1, 0))
+        fits = fits * ((before <= limits[group]) & (count_obs - before <= limits[groups - 2 - group])).astype(i32)
+    fits_ref[0] = fits
     values = packed[:, :size]
     extras = packed[:, size:]
     codes_down = extras[:, 0:1].astype(i32)
@@ -203,9 +215,10 @@
             jax.ShapeDtypeStruct((row_blocks, size, count_obs), f32),
             jax.ShapeDtypeStruct((col_blocks, count_obs, size), f32),
             jax.ShapeDtypeStruct((count_obs, count_obs), f32),
+            jax.ShapeDtypeStruct((1,), i32),
         ),
         in_specs=[SMEM, VMEM, ANY],
-        out_specs=(VMEM, VMEM, VMEM),
+        out_specs=(VMEM, VMEM, VMEM, SMEM),
         scratch_shapes=[
             pltpu.SMEM((tiles,), i32),
             pltpu.SMEM((row_blocks * windows,), i32),
@@ -470,7 +483,7 @@
 
 
 def exchange_kernel(
-    count_bits, row_ref, col_ref, gram_ref, rows_out, cols_out, inverse_out,
+    count_bits, limits, row_ref, col_ref, gram_ref, rows_out, cols_out, inverse_out,
     gram_out, work, send, recv, from_core, sums, landed, upward, downward, rows_here, cols_here, total, relay,
     gram_work, gram_core, gram_bits, gram_line,
 ):
@@ -514,56 +527,76 @@
 
     up, down = sems.take(line), sems.take(line)
 
+    many_obs = total.shape[0]
+
+    def up_rows(place):
+        return pl.ds(0, limits[place])
+
+    def down_rows(place):
+        return pl.ds(many_obs - limits[line - 1 - place], limits[line - 1 - place])
+
+    def up_copy(place, chunk, source):
+        rows = up_rows(place)
+        return copy(source.at[chunk, rows], upward.at[chunk, rows], up + chunk, (z + 1, j))
+
+    def down_copy(place, chunk, source):
+        rows = down_rows(place)
+        return copy(source.at[chunk, rows], downward.at[chunk, rows], down + chunk, (z - 1, j))
+
     def line_begin(step):
-        chunk, other = line - step, step - 1
-
         @pl.when(z == 0)
         def _():
-            copy(col_ref.at[chunk], upward.at[chunk], up + chunk, (z + 1, j)).start()
+            up_copy(0, line - step, col_ref).start()
 
         @pl.when(z == line - 1)
         def _():
-            copy(col_ref.at[other], downward.at[other], down + other, (z - 1, j)).start()
+            down_copy(line - 1, step - 1, col_ref).start()
 
     def line_round(step):
-        chunk, other = z + line - 1 - step, z - line + 1 + step
-
-        @pl.when((z > 0) & (chunk < line))
-        def _():
-            copy(upward.at[chunk], upward.at[chunk], up + chunk).wait_recv()
-            upward[chunk] += col_ref[chunk]
-            copy(upward.at[chunk], upward.at[chunk], up + chunk, (z + 1, j)).start()
-
-        @pl.when((z < line - 1) & (other >= 0))
-        def _():
-            copy(downward.at[other], downward.at[other], down + other).wait_recv()
-            downward[other] += col_ref[other]
-            copy(downward.at[other], downward.at[other], down + other, (z - 1, j)).start()
+        for place in range(1, line - 1):
+            chunk, other = place + line - 1 - step, place - line + 1 + step
+
+            @pl.when(z == place)
+            def _():
+                if chunk < line:
+                    fresh = limits[place] - limits[place - 1]
+                    up_copy(place - 1, chunk, upward).wait_recv()
+                    upward[chunk, up_rows(place - 1)] += col_ref[chunk, up_rows(place - 1)]
+                    if fresh:
+                        later = pl.ds(limits[place - 1], fresh)
+                        upward[chunk, later] = col_ref[chunk, later]
+                    up_copy(place, chunk, upward).start()
+                if other >= 0:
+                    fresh = limits[line - 1 - place] - limits[line - 2 - place]
+                    down_copy(place + 1, other, downward).wait_recv()
+                    downward[other, down_rows(place + 1)] += col_ref[other, down_rows(place + 1)]
+                    if fresh:
+                        later = pl.ds(many_obs - limits[line - 1 - place], fresh)
+                        downward[other, later] = col_ref[other, later]
+                    down_copy(place, other, downward).start()
 
     def line_end():
         total[...] = col_ref[z]
-
-        @pl.when(z > 0)
-        def _():
-            copy(upward.at[z], upward.at[z], up + z).wait_recv()
-            total[...] += upward[z]
-
-        @pl.when(z < line - 1)
-        def _():
-            copy(downward.at[z], downward.at[z], down + z).wait_recv()
-            total[...] += downward[z]
+        for place in range(line):
+
+            @pl.when(z == place)
+            def _():
+                if place > 0:
+                    up_copy(place - 1, place, upward).wait_recv()
+                    total[up_rows(place - 1)] += upward[place, up_rows(place - 1)]
+                if place < line - 1:
+                    down_copy(place + 1, place, downward).wait_recv()
+                    total[down_rows(place + 1)] += downward[place, down_rows(place + 1)]
 
     def line_sent():
-        for step in range(1, line):
-            chunk, other = line - step, step - 1
-
-            @pl.when(z < chunk)
-            def _():
-                copy(upward.at[chunk], upward.at[chunk], up + chunk).wait_send()
-
-            @pl.when(z > other)
-            def _():
-                copy(downward.at[other], downward.at[other], down + other).wait_send()
+        for place in range(line):
+
+            @pl.when(z == place)
+            def _():
+                for chunk in range(place + 1, line):
+                    up_copy(place, chunk, upward).wait_send()
+                for other in range(place):
+                    down_copy(place, other, downward).wait_send()
 
     def chosen(part, step, flip):
         order = [(part + turn) % count_bits for turn in range(count_bits)]
@@ -603,7 +636,8 @@
             for slot, pick in enumerate(picks):
                 sums[pick, part] += landed[step_base[step] + part * len(picks) + slot]
 
-    line_begin(1)
+    for step in range(1, line):
+        line_begin(step)
     held = 2**count_bits
     half = begin(gram_ref.at[pl.ds((1 - core) * held, held)], gram_core, beside)
     core_sum = begin(row_ref.at[1 - core], from_core, beside)
@@ -620,9 +654,6 @@
     base = sems.take(line)
     for step in range(1, line):
         copy(gram_work.at[mine], gram_line.at[z], base + step, (lax.rem(z + step, line), j)).start()
-    for step in range(2, line):
-        line_begin(step)
-
     core_sum.wait_recv()
     for owner in range(line):
         chunk = mixed(owner, z)
@@ -644,6 +675,23 @@
         yield
         sent.wait_recv()
 
+    to_cols, first_leg, second_leg = sems.take(), sems.take(2), sems.take(2)
+    owned = mixed(chip, z)
+    apart = (owned != z) | (z != chip)
+    column = (owned, 2 * z + core)
+    via = mixed(z, chip)
+    beyond = plane_of(chip, z)
+
+    def piece(ref, number):
+        size = total.shape[0] // 2
+        return ref.at[pl.ds(number * size, size)]
+
+    def leg_one(number):
+        return copy(piece(total, number), piece(relay, number), first_leg + number, (z, 2 * via + core))
+
+    def leg_two(number):
+        return copy(piece(relay, number), piece(cols_here, number), second_leg + number, (beyond, j))
+
     gram_turns = gram_back()
     for step in range(1, line - 1):
         line_round(step)
@@ -652,45 +700,10 @@
             plane_add(step - 1, made)
             made = plane_send(step)
             next(gram_turns, None)
-    for _ in gram_turns:
-        pass
     for step in range(max(line - 1, 1), count_bits):
         plane_add(step - 1, made)
         made = plane_send(step)
-    plane_add(count_bits - 1, made)
-    inverse_turns = inverse_steps(gram_out, inverse_out, work)
-
-    def fill(number):
-        for _ in range(number):
-            next(inverse_turns, None)
-
-    to_cols, first_leg, second_leg = sems.take(), sems.take(2), sems.take(2)
-    owned = mixed(chip, z)
-    apart = (owned != z) | (z != chip)
-    column = (owned, 2 * z + core)
-    via = mixed(z, chip)
-    beyond = plane_of(chip, z)
-
-    @pl.when(apart)
-    def _():
-        copy(sums.at[chip], rows_here, to_cols, column).start()
-
-    @pl.when(jnp.logical_not(apart))
-    def _():
-        rows_here[...] = sums[chip]
-
-    fill(1)
     line_end()
-
-    def piece(ref, number):
-        size = total.shape[0] // 2
-        return ref.at[pl.ds(number * size, size)]
-
-    def leg_one(number):
-        return copy(piece(total, number), piece(relay, number), first_leg + number, (z, 2 * via + core))
-
-    def leg_two(number):
-        return copy(piece(relay, number), piece(cols_here, number), second_leg + number, (beyond, j))
 
     @pl.when(via != chip)
     def _():
@@ -701,6 +714,39 @@
     def _():
         relay[...] = total[...]
 
+    for _ in gram_turns:
+        pass
+    plane_add(count_bits - 1, made)
+    inverse_turns = inverse_steps(gram_out, inverse_out, work)
+
+    def fill(number):
+        for _ in range(number):
+            next(inverse_turns, None)
+
+    @pl.when(apart)
+    def _():
+        copy(sums.at[chip], rows_here, to_cols, column).start()
+
+    @pl.when(jnp.logical_not(apart))
+    def _():
+        rows_here[...] = sums[chip]
+
+    for number in range(2):
+
+        @pl.when(via != chip)
+        def _():
+            leg_one(number).wait()
+
+        @pl.when(beyond != z)
+        def _():
+            leg_two(number).start()
+
+    @pl.when(beyond == z)
+    def _():
+        cols_here[...] = relay[...]
+
+    fill(2)
+
     @pl.when(apart)
     def _():
         copy(sums.at[chip], rows_here, to_cols, column).wait()
@@ -744,21 +790,7 @@
                 copy(cols_out.at[other], cols_out.at[other], back + other).wait_send()
 
     line_spread(1)
-    for number in range(2):
-
-        @pl.when(via != chip)
-        def _():
-            leg_one(number).wait()
-
-        @pl.when(beyond != z)
-        def _():
-            leg_two(number).start()
-
-    @pl.when(beyond == z)
-    def _():
-        cols_here[...] = relay[...]
-
-    fill(3)
+    fill(1)
 
     @pl.when(beyond != z)
     def _():
@@ -797,7 +829,7 @@
         one.wait_send()
 
 
-def exchange(row_part, col_part, gram_part):
+def exchange(limits, row_part, col_part, gram_part):
     line, many = lax.axis_size("tr"), lax.axis_size("tc")
     count_bits = line.bit_length() - 1
     row_blocks, size, count_obs = row_part.shape
@@ -809,7 +841,7 @@
     landings = sum(parts * 2 ** (count_bits - 1 - step) for step in range(count_bits))
     part = pivot_size(count_obs)
     cross_rows, cross_cols, inverted = pl.pallas_call(
-        functools.partial(exchange_kernel, count_bits),
+        functools.partial(exchange_kernel, count_bits, limits),
         out_shape=tuple(jax.ShapeDtypeStruct(shape, f32) for shape in (rows, cols, gram_part.shape)),
         in_specs=[VMEM] * 3,
         out_specs=(VMEM,) * 3,
@@ -842,11 +874,20 @@
     size = obs_values.shape[2]
     line, many = lax.axis_size("tr"), lax.axis_size("tc")
     packed = share(pack(stations, obs_values, obs_error))
-    row_part, col_part, gram_part = forward(block_order, packed, cov_tiles, size)
+    row_part, col_part, gram_part, fits = forward(block_order, packed, cov_tiles, size)
     square = many == 2 * line and line & (line - 1) == 0 and line > 1
     whole_tiles = row_part.shape[0] == many and col_part.shape[0] == line
-    spread = exchange if square and whole_tiles else exchange_plain
-    cross_rows, cross_cols, inverted = spread(row_part, col_part, gram_part)
+    parts = (row_part, col_part, gram_part)
+    if square and whole_tiles:
+        count_obs = gram_part.shape[0]
+        cross_rows, cross_cols, inverted = lax.cond(
+            fits[0] > 0,
+            functools.partial(exchange, reach(count_obs, line)),
+            functools.partial(exchange, (count_obs,) * line),
+            *parts,
+        )
+    else:
+        cross_rows, cross_cols, inverted = exchange_plain(*parts)
     return update(block_order, cross_rows, cross_cols, inverted, cov_tiles)
 
 

time: 188 us -> 184 us (0.979)
  Pallas kernels: 184 us -> 179 us
    pallas_call x1, Pallas kernels: 115 us -> 112 us  [exchange(): pl.pallas_call(functools.partial(exchange_kernel, count_bits, limits), ou...]
    pallas_call x1, Pallas kernels: 29.6 us -> 27.3 us  [forward(): pl.pallas_call(forward_kernel, out_shape=(jax.ShapeDtypeStruct((row_block...]
where the time goes in v5:
time: 184 us; the launch traced here: 183 us
  Pallas kernels  179 us (97%)
  other arithmetic  2.21 us (1%)
    pallas_call x1, Pallas kernels, exchange(): pl.pallas_call(functools.partial(exchange_kernel, count_bits, limits), ou...  112 us
    pallas_call x1, Pallas kernels, forward(): pl.pallas_call(forward_kernel, out_shape=(jax.ShapeDtypeStruct((row_block...  27.3 us
    pallas_call x1, Pallas kernels, update(): pl.pallas_call(update_kernel, out_shape=jax.ShapeDtypeStruct(cov_tiles.sh...  23.4 us
    pallas_call x1, Pallas kernels, share(): pl.pallas_call(share_kernel, out_shape=jax.ShapeDtypeStruct((many, *packe...  16.4 us

profile of v5, /device:TPU:0, one launch (start us, length us, event | category | flops | bytes accessed | tf_op | source)
XLA Modules:
  0.0 182.9 jit_solution(10240205098988011599)
XLA Ops:
  0.0 0.7 convert_bitcast_fusion
  0.7 0.1 pad.3.clone
  0.7 0.1 copy.6
  0.8 0.7 copy.7
  1.6 1.6 maximum_maximum_fusion.mine_ref
  3.1 16.4 %share.1 = f32[8,32,640]{2,1,0:T(8,128)} custom-call(f32[32,640]{1,0:T(8,128)} %maximum_maximum_fusion.mine_ref), custom_call_target="tpu_custom_call" | custom-call | tf_op jit(solution)/shard_map/share/pallas_call | solution.py:473
  19.5 27.3 %forward.1 = (f32[8,512,256]{2,1,0:T(8,128)}, f32[4,256,512]{2,1,0:T(8,128)S(1)}, f32[256,256]{1,0:T(8,128)S(1)}, s32[1]{0:T(128)}) custom-call(s32[32]{0:T(128)} %order_ref.3, f32[256,640]{1,0:T(8,128)} %bitcast.18, f32[4096,2048]{1,0:T(8,128)} %cov_ref.3), custom_call_target="tpu_custom_call" | custom-call | flops 12884901888 | bytes 16777216 | tf_op jit(solution)/shard_map/forward/pallas_call | solution.py:212
  47.4 111.9 %conditional.1 = (f32[8,512,256]{2,1,0:T(8,128)}, f32[4,256,512]{2,1,0:T(8,128)}, f32[256,256]{1,0:T(8,128)S(1)}) conditional(s32[]{:T(128)} %bitcast.10, (f32[8,512,256]{2,1,0:T(8,128)}, f32[256,256]{1,0:T(8,128)S(1)}, f32[4,256,512]{2,1,0:T(8,128)S(1)}) %tuple.13, (f32[8,512,256]{2,1,0:T(8,128)}, f32[256,256]{1,0:T(8,128)S(1)}, ...), branch_computations={%region_0.0_spmd, %region_1.0_spmd} | conditional | bytes 24 | solution.py:883
  47.4 111.7 %exchange.3 = (f32[2,4,2,256,256]{4,3,2,1,0:T(8,128)}, f32[4,256,512]{2,1,0:T(8,128)}, f32[256,256]{1,0:T(8,128)S(1)}) custom-call(f32[2,4,2,256,256]{4,3,2,1,0:T(8,128)} %bitcast.13, f32[4,256,512]{2,1,0:T(8,128)S(1)} %get-tuple-element.24.col_ref, f32[8,32,256]{2,1,0:T(8,128)S(1)} %bitcast.17), custom_call_target="tpu_custom_call" | custom-call | tf_op jit(solution)/shard_map/cond/branch_1_fun/exchange/pallas_call | solution.py:843
  159.3 23.4 %update.1 = f32[4096,2048]{1,0:T(8,128)} custom-call(s32[32]{0:T(128)} %order_ref.3, f32[8,512,256]{2,1,0:T(8,128)} %get-tuple-element.40.rows_ref, f32[4,256,512]{2,1,0:T(8,128)} %get-tuple-element.41.cols_ref, f32[256,256]{1,0:T(8,128)S(1)} %get-tuple-element.42.inverse_ref, f32[4096,2048]{1,0:T(8,128)} %cov_ref.3), custom_call_target="tpu_custom_call" | custom-call | flops 6442450944 | bytes 50331648 | tf_op jit(solution)/shard_map/update/pallas_call | solution.py:301
  (1 shorter events, 0.0 us)

commit v6 on v5

--- a/solution.py
+++ b/solution.py
@@ -10,6 +10,7 @@
 exact = lax.Precision.HIGHEST
 bf16, f32, i32 = jnp.bfloat16, jnp.float32, jnp.int32
 DEPTH = 4
+ROOM = 40 * 2**20
 ANY = pl.BlockSpec(memory_space=pl.ANY)
 VMEM = pl.BlockSpec(memory_space=pltpu.VMEM)
 SMEM = pl.BlockSpec(memory_space=pltpu.SMEM)
@@ -231,6 +232,7 @@
         cost_estimate=pl.CostEstimate(
             flops=6 * tiles * size * size * count_obs, bytes_accessed=2 * tiles * size * size, transcendentals=0
         ),
+        compiler_params=pltpu.CompilerParams(vmem_limit_bytes=ROOM),
         name="forward",
     )(block_order, packed, cov_tiles)
 
@@ -316,6 +318,7 @@
         cost_estimate=pl.CostEstimate(
             flops=3 * tiles * size * size * count_obs, bytes_accessed=6 * tiles * size * size, transcendentals=0
         ),
+        compiler_params=pltpu.CompilerParams(vmem_limit_bytes=ROOM),
         name="update",
     )(block_order, cross_rows, cross_cols, inverted, cov_tiles)
 
@@ -388,20 +391,6 @@
         cost_estimate=pl.CostEstimate(flops=400_000_000, bytes_accessed=8 * size * size, transcendentals=0),
         name="inverse",
     )(matrix)
-
-
-def pack(stations, obs_values, obs_error):
-    values = obs_values[0]
-    count, size = values.shape
-    return jnp.concatenate(
-        (
-            values,
-            stations[0].astype(f32)[:, None],
-            obs_error[0][:, None],
-            jnp.zeros((count, 126), f32),
-        ),
-        axis=1,
-    )
 
 
 def exchange_plain(row_part, col_part, gram_part):
@@ -435,7 +424,7 @@
         return self.count - number
 
 
-def share_kernel(mine_ref, all_ref, send, recv, core_send, core_recv):
+def share_kernel(stations_ref, values_ref, errors_ref, all_ref, mine_ref, send, recv, core_send, core_recv):
     row, col = lax.axis_index("tr"), lax.axis_index("tc")
     chips = all_ref.shape[0] // 2
     chip, core = col // 2, col % 2
@@ -452,6 +441,16 @@
             device_id=(row, 2 * chip + 1 - core), device_id_type=pl.DeviceIdType.MESH,
         )
 
+    number, size = values_ref.shape[1:]
+    equal = lax.broadcasted_iota(i32, (number, number), 0) == lax.broadcasted_iota(i32, (number, number), 1)
+
+    def upright(across):
+        return jnp.sum(jnp.where(equal, across, 0.0), axis=1, keepdims=True)
+
+    lanes = lax.broadcasted_iota(i32, (number, mine_ref.shape[1] - size), 1)
+    stations, errors = upright(stations_ref[...].astype(f32)), upright(errors_ref[...])
+    mine_ref[:, :size] = values_ref[0]
+    mine_ref[:, size:] = jnp.where(lanes == 0, stations, jnp.where(lanes == 1, errors, 0.0))
     sent = [copy(mine_ref, col, step) for step in range(1, chips)]
     sent.append(beside(mine_ref, col, 0))
     for one in sent:
@@ -468,18 +467,20 @@
         one.wait_send()
 
 
-def share(packed):
+def share(stations, obs_values, obs_error):
     many = lax.axis_size("tc")
+    _, number, size = obs_values.shape
+    packed = (number, size + 128)
     full = pl.pallas_call(
         share_kernel,
-        out_shape=jax.ShapeDtypeStruct((many, *packed.shape), f32),
-        in_specs=[VMEM],
+        out_shape=jax.ShapeDtypeStruct((many, *packed), f32),
+        in_specs=[VMEM] * 3,
         out_specs=VMEM,
-        scratch_shapes=[pltpu.SemaphoreType.DMA((many // 2,))] * 4,
-        compiler_params=pltpu.CompilerParams(has_side_effects=True),
+        scratch_shapes=[pltpu.VMEM(packed, f32)] + [pltpu.SemaphoreType.DMA((many // 2,))] * 4,
+        compiler_params=pltpu.CompilerParams(has_side_effects=True, vmem_limit_bytes=8 * 2**20),
         name="share",
-    )(packed)
-    return full.reshape(many * packed.shape[0], packed.shape[1])
+    )(stations, obs_values, obs_error)
+    return full.reshape(many * number, size + 128)
 
 
 def exchange_kernel(
@@ -864,7 +865,7 @@
             pltpu.VMEM((many // 2, seg, count_obs), f32),
             pltpu.VMEM((line, seg, count_obs), f32),
         ],
-        compiler_params=pltpu.CompilerParams(has_side_effects=True),
+        compiler_params=pltpu.CompilerParams(has_side_effects=True, vmem_limit_bytes=ROOM),
         name="exchange",
     )(row_part.reshape(rows), col_part, gram_part.reshape(gram))
     return cross_rows.reshape(row_part.shape), cross_cols, inverted
@@ -873,7 +874,7 @@
 def body(cov_tiles, block_order, stations, obs_values, obs_error):
     size = obs_values.shape[2]
     line, many = lax.axis_size("tr"), lax.axis_size("tc")
-    packed = share(pack(stations, obs_values, obs_error))
+    packed = share(stations, obs_values, obs_error)
     row_part, col_part, gram_part, fits = forward(block_order, packed, cov_tiles, size)
     square = many == 2 * line and line & (line - 1) == 0 and line > 1
     whole_tiles = row_part.shape[0] == many and col_part.shape[0] == line

time: 184 us -> 175 us (0.951)
  Pallas kernels: 179 us -> 171 us
  other arithmetic: 2.21 us -> 0 us
  local copies, waits for them, and re-layouts: 0.9 us -> 2.81 us
    unnamed x0 -> x10, local copies, waits for them, and re-layouts: none -> 2.81 us
    pallas_call x1, Pallas kernels: 112 us -> 109 us  [exchange(): pl.pallas_call(functools.partial(exchange_kernel, count_bits, limits), ou...]
    pallas_call x1, Pallas kernels: 23.4 us -> 21.4 us  [update(): pl.pallas_call(update_kernel, out_shape=jax.ShapeDtypeStruct(cov_tiles.sh...]
where the time goes in v6:
time: 175 us
  Pallas kernels  171 us (98%)
  local copies, waits for them, and re-layouts  2.81 us (2%)
    pallas_call x1, Pallas kernels, exchange(): pl.pallas_call(functools.partial(exchange_kernel, count_bits, limits), ou...  109 us
    pallas_call x1, Pallas kernels, forward(): pl.pallas_call(forward_kernel, out_shape=(jax.ShapeDtypeStruct((row_block...  26.2 us
    pallas_call x1, Pallas kernels, update(): pl.pallas_call(update_kernel, out_shape=jax.ShapeDtypeStruct(cov_tiles.sh...  21.4 us
    pallas_call x1, Pallas kernels, share(): pl.pallas_call(share_kernel, out_shape=jax.ShapeDtypeStruct((many, *packe...  14.7 us

profile of v6, /device:TPU:0, one launch (start us, length us, event | category | flops | bytes accessed | tf_op | source)
XLA Modules:
  0.0 175.2 jit_solution(10982152291372890235)
XLA Ops:
  0.0 0.0 copy-start
  0.0 0.8 copy-done
  0.8 0.0 copy-start.1
  0.8 0.7 copy-done.1
  1.5 0.0 copy-start.2
  1.5 0.7 copy-done.2
  2.2 14.7 %share.1 = f32[8,32,640]{2,1,0:T(8,128)S(1)} custom-call(s32[1,32]{1,0:T(1,128)S(1)} %copy-done.1, f32[1,32,512]{2,1,0:T(8,128)S(1)} %copy-done, f32[1,32]{1,0:T(1,128)S(1)} %copy-done.2), custom_call_target="tpu_custom_call" | custom-call | tf_op jit(solution)/shard_map/share/pallas_call | solution.py:474
  16.9 0.0 copy-start.3
  16.9 0.6 copy-done.3
  17.5 26.2 %forward.1 = (f32[8,512,256]{2,1,0:T(8,128)S(1)}, f32[4,256,512]{2,1,0:T(8,128)S(1)}, f32[256,256]{1,0:T(8,128)S(1)}, s32[1]{0:T(128)}) custom-call(s32[32]{0:T(128)S(1)} %copy-done.3, f32[256,640]{1,0:T(8,128)S(1)} %bitcast.8, f32[4096,2048]{1,0:T(8,128)} %cov_ref.3), custom_call_target="tpu_custom_call" | custom-call | flops 12884901888 | bytes 16777216 | tf_op jit(solution)/shard_map/forward/pallas_call | solution.py:213
  44.4 0.0 copy-start.4
  44.4 109.2 %conditional.1 = (f32[8,512,256]{2,1,0:T(8,128)S(1)}, f32[4,256,512]{2,1,0:T(8,128)S(1)}, f32[256,256]{1,0:T(8,128)S(1)}) conditional(s32[]{:T(128)} %bitcast.7, (f32[8,512,256]{2,1,0:T(8,128)S(1)}, f32[256,256]{1,0:T(8,128)S(1)}, f32[4,256,512]{2,1,0:T(8,128)S(1)}) %tuple.13, (f32[8,512,256]{2,1,0:T(8,128)S(1)}, f32[256,256]{1,0:T(8,128)S(1)}, ...), branch_computations={%region_0.0_spmd, %region_1.0_spmd} | conditional | bytes 24 | solution.py:884
  44.4 109.0 %exchange.3 = (f32[2,4,2,256,256]{4,3,2,1,0:T(8,128)S(1)}, f32[4,256,512]{2,1,0:T(8,128)S(1)}, f32[256,256]{1,0:T(8,128)S(1)}) custom-call(f32[2,4,2,256,256]{4,3,2,1,0:T(8,128)S(1)} %bitcast.10, f32[4,256,512]{2,1,0:T(8,128)S(1)} %get-tuple-element.24.col_ref, f32[8,32,256]{2,1,0:T(8,128)S(1)} %bitcast.14), custom_call_target="tpu_custom_call" | custom-call | tf_op jit(solution)/shard_map/cond/branch_1_fun/exchange/pallas_call | solution.py:844
  153.6 0.0 copy-done.4
  153.6 21.4 %update.1 = f32[4096,2048]{1,0:T(8,128)} custom-call(s32[32]{0:T(128)S(1)} %copy-done.4, f32[8,512,256]{2,1,0:T(8,128)S(1)} %get-tuple-element.40.rows_ref, f32[4,256,512]{2,1,0:T(8,128)S(1)} %get-tuple-element.41.cols_ref, f32[256,256]{1,0:T(8,128)S(1)} %get-tuple-element.42.inverse_ref, f32[4096,2048]{1,0:T(8,128)} %cov_ref.3), custom_call_target="tpu_custom_call" | custom-call | flops 6442450944 | bytes 50331648 | tf_op jit(solution)/shard_map/update/pallas_call | solution.py:303
Async XLA Ops:
  0.0 0.8 copy-start
  0.8 0.7 copy-start.1
  1.5 0.7 copy-start.2
  16.9 0.7 copy-start.3
  44.4 109.2 %copy-start.4 = (s32[32]{0:T(128)S(1)}, s32[32]{0:T(128)}, u32[]{:S(2)}) copy-start(s32[32]{0:T(128)} %order_ref.3) | copy-start | bytes 388

commit v7 on v6

--- a/solution.py
+++ b/solution.py
@@ -746,7 +746,7 @@
     def _():
         cols_here[...] = relay[...]
 
-    fill(2)
+    fill(1)
 
     @pl.when(apart)
     def _():
@@ -791,7 +791,7 @@
                 copy(cols_out.at[other], cols_out.at[other], back + other).wait_send()
 
     line_spread(1)
-    fill(1)
+    fill(2)
 
     @pl.when(beyond != z)
     def _():

time: 175 us -> 176 us (level)
  the two profiles are of different devices: /device:TPU:0 before, /device:TPU:4 now
where the time goes in v7:
time: 176 us; the launch traced here: 177 us
  Pallas kernels  173 us (98%)
  local copies, waits for them, and re-layouts  2.81 us (2%)
    pallas_call x1, Pallas kernels, exchange(): pl.pallas_call(functools.partial(exchange_kernel, count_bits, limits), ou...  99.8 us
    pallas_call x1, Pallas kernels, forward(): pl.pallas_call(forward_kernel, out_shape=(jax.ShapeDtypeStruct((row_block...  35.4 us
    pallas_call x1, Pallas kernels, update(): pl.pallas_call(update_kernel, out_shape=jax.ShapeDtypeStruct(cov_tiles.sh...  25 us
    pallas_call x1, Pallas kernels, share(): pl.pallas_call(share_kernel, out_shape=jax.ShapeDtypeStruct((many, *packe...  13.1 us

profile of v7, /device:TPU:4, one launch (start us, length us, event | category | flops | bytes accessed | tf_op | source)
XLA Modules:
  0.0 177.2 jit_solution(14762087559745139543)
XLA Ops:
  0.0 0.0 copy-start
  0.0 0.8 copy-done
  0.8 0.0 copy-start.1
  0.8 0.7 copy-done.1
  1.5 0.0 copy-start.2
  1.5 0.7 copy-done.2
  2.2 13.1 %share.1 = f32[8,32,640]{2,1,0:T(8,128)S(1)} custom-call(s32[1,32]{1,0:T(1,128)S(1)} %copy-done.1, f32[1,32,512]{2,1,0:T(8,128)S(1)} %copy-done, f32[1,32]{1,0:T(1,128)S(1)} %copy-done.2), custom_call_target="tpu_custom_call" | custom-call | tf_op jit(solution)/shard_map/share/pallas_call | solution.py:474
  15.3 0.0 copy-start.3
  15.3 0.6 copy-done.3
  15.9 35.4 %forward.1 = (f32[8,512,256]{2,1,0:T(8,128)S(1)}, f32[4,256,512]{2,1,0:T(8,128)S(1)}, f32[256,256]{1,0:T(8,128)S(1)}, s32[1]{0:T(128)}) custom-call(s32[32]{0:T(128)S(1)} %copy-done.3, f32[256,640]{1,0:T(8,128)S(1)} %bitcast.8, f32[4096,2048]{1,0:T(8,128)} %cov_ref.3), custom_call_target="tpu_custom_call" | custom-call | flops 12884901888 | bytes 16777216 | tf_op jit(solution)/shard_map/forward/pallas_call | solution.py:213
  52.0 0.0 copy-start.4
  52.0 100.0 %conditional.1 = (f32[8,512,256]{2,1,0:T(8,128)S(1)}, f32[4,256,512]{2,1,0:T(8,128)S(1)}, f32[256,256]{1,0:T(8,128)S(1)}) conditional(s32[]{:T(128)} %bitcast.7, (f32[8,512,256]{2,1,0:T(8,128)S(1)}, f32[256,256]{1,0:T(8,128)S(1)}, f32[4,256,512]{2,1,0:T(8,128)S(1)}) %tuple.13, (f32[8,512,256]{2,1,0:T(8,128)S(1)}, f32[256,256]{1,0:T(8,128)S(1)}, ...), branch_computations={%region_0.0_spmd, %region_1.0_spmd} | conditional | bytes 24 | solution.py:884
  52.1 99.8 %exchange.3 = (f32[2,4,2,256,256]{4,3,2,1,0:T(8,128)S(1)}, f32[4,256,512]{2,1,0:T(8,128)S(1)}, f32[256,256]{1,0:T(8,128)S(1)}) custom-call(f32[2,4,2,256,256]{4,3,2,1,0:T(8,128)S(1)} %bitcast.10, f32[4,256,512]{2,1,0:T(8,128)S(1)} %get-tuple-element.24.col_ref, f32[8,32,256]{2,1,0:T(8,128)S(1)} %bitcast.14), custom_call_target="tpu_custom_call" | custom-call | tf_op jit(solution)/shard_map/cond/branch_1_fun/exchange/pallas_call | solution.py:844
  152.1 0.0 copy-done.4
  152.1 25.0 %update.1 = f32[4096,2048]{1,0:T(8,128)} custom-call(s32[32]{0:T(128)S(1)} %copy-done.4, f32[8,512,256]{2,1,0:T(8,128)S(1)} %get-tuple-element.40.rows_ref, f32[4,256,512]{2,1,0:T(8,128)S(1)} %get-tuple-element.41.cols_ref, f32[256,256]{1,0:T(8,128)S(1)} %get-tuple-element.42.inverse_ref, f32[4096,2048]{1,0:T(8,128)} %cov_ref.3), custom_call_target="tpu_custom_call" | custom-call | flops 6442450944 | bytes 50331648 | tf_op jit(solution)/shard_map/update/pallas_call | solution.py:303
Async XLA Ops:
  0.0 0.8 copy-start
  0.8 0.7 copy-start.1
  1.5 0.7 copy-start.2
  15.3 0.7 copy-start.3
  52.0 100.0 %copy-start.4 = (s32[32]{0:T(128)S(1)}, s32[32]{0:T(128)}, u32[]{:S(2)}) copy-start(s32[32]{0:T(128)} %order_ref.3) | copy-start | bytes 388

commit v8 on v7

--- a/solution.py
+++ b/solution.py
@@ -746,8 +746,6 @@
     def _():
         cols_here[...] = relay[...]
 
-    fill(1)
-
     @pl.when(apart)
     def _():
         copy(sums.at[chip], rows_here, to_cols, column).wait()
@@ -791,7 +789,7 @@
                 copy(cols_out.at[other], cols_out.at[other], back + other).wait_send()
 
     line_spread(1)
-    fill(2)
+    fill(3)
 
     @pl.when(beyond != z)
     def _():

time: 176 us -> 173 us (0.983)
  the two profiles are of different devices: /device:TPU:4 before, /device:TPU:5 now
where the time goes in v8:
time: 173 us
  Pallas kernels  169 us (98%)
  local copies, waits for them, and re-layouts  2.81 us (2%)
    pallas_call x1, Pallas kernels, exchange(): pl.pallas_call(functools.partial(exchange_kernel, count_bits, limits), ou...  102 us
    pallas_call x1, Pallas kernels, forward(): pl.pallas_call(forward_kernel, out_shape=(jax.ShapeDtypeStruct((row_block...  31.1 us
    pallas_call x1, Pallas kernels, update(): pl.pallas_call(update_kernel, out_shape=jax.ShapeDtypeStruct(cov_tiles.sh...  22.7 us
    pallas_call x1, Pallas kernels, share(): pl.pallas_call(share_kernel, out_shape=jax.ShapeDtypeStruct((many, *packe...  13.7 us

profile of v8, /device:TPU:5, one launch (start us, length us, event | category | flops | bytes accessed | tf_op | source)
XLA Modules:
  0.0 173.2 jit_solution(10561203558391218346)
XLA Ops:
  0.0 0.0 copy-start
  0.0 0.8 copy-done
  0.8 0.0 copy-start.1
  0.8 0.7 copy-done.1
  1.5 0.0 copy-start.2
  1.5 0.7 copy-done.2
  2.2 13.7 %share.1 = f32[8,32,640]{2,1,0:T(8,128)S(1)} custom-call(s32[1,32]{1,0:T(1,128)S(1)} %copy-done.1, f32[1,32,512]{2,1,0:T(8,128)S(1)} %copy-done, f32[1,32]{1,0:T(1,128)S(1)} %copy-done.2), custom_call_target="tpu_custom_call" | custom-call | tf_op jit(solution)/shard_map/share/pallas_call | solution.py:474
  15.8 0.0 copy-start.3
  15.8 0.6 copy-done.3
  16.5 31.1 %forward.1 = (f32[8,512,256]{2,1,0:T(8,128)S(1)}, f32[4,256,512]{2,1,0:T(8,128)S(1)}, f32[256,256]{1,0:T(8,128)S(1)}, s32[1]{0:T(128)}) custom-call(s32[32]{0:T(128)S(1)} %copy-done.3, f32[256,640]{1,0:T(8,128)S(1)} %bitcast.8, f32[4096,2048]{1,0:T(8,128)} %cov_ref.3), custom_call_target="tpu_custom_call" | custom-call | flops 12884901888 | bytes 16777216 | tf_op jit(solution)/shard_map/forward/pallas_call | solution.py:213
  48.2 0.0 copy-start.4
  48.2 102.1 %conditional.1 = (f32[8,512,256]{2,1,0:T(8,128)S(1)}, f32[4,256,512]{2,1,0:T(8,128)S(1)}, f32[256,256]{1,0:T(8,128)S(1)}) conditional(s32[]{:T(128)} %bitcast.7, (f32[8,512,256]{2,1,0:T(8,128)S(1)}, f32[256,256]{1,0:T(8,128)S(1)}, f32[4,256,512]{2,1,0:T(8,128)S(1)}) %tuple.13, (f32[8,512,256]{2,1,0:T(8,128)S(1)}, f32[256,256]{1,0:T(8,128)S(1)}, ...), branch_computations={%region_0.0_spmd, %region_1.0_spmd} | conditional | bytes 24 | solution.py:882
  48.2 101.9 %exchange.3 = (f32[2,4,2,256,256]{4,3,2,1,0:T(8,128)S(1)}, f32[4,256,512]{2,1,0:T(8,128)S(1)}, f32[256,256]{1,0:T(8,128)S(1)}) custom-call(f32[2,4,2,256,256]{4,3,2,1,0:T(8,128)S(1)} %bitcast.10, f32[4,256,512]{2,1,0:T(8,128)S(1)} %get-tuple-element.24.col_ref, f32[8,32,256]{2,1,0:T(8,128)S(1)} %bitcast.14), custom_call_target="tpu_custom_call" | custom-call | tf_op jit(solution)/shard_map/cond/branch_1_fun/exchange/pallas_call | solution.py:842
  150.4 0.0 copy-done.4
  150.4 22.7 %update.1 = f32[4096,2048]{1,0:T(8,128)} custom-call(s32[32]{0:T(128)S(1)} %copy-done.4, f32[8,512,256]{2,1,0:T(8,128)S(1)} %get-tuple-element.40.rows_ref, f32[4,256,512]{2,1,0:T(8,128)S(1)} %get-tuple-element.41.cols_ref, f32[256,256]{1,0:T(8,128)S(1)} %get-tuple-element.42.inverse_ref, f32[4096,2048]{1,0:T(8,128)} %cov_ref.3), custom_call_target="tpu_custom_call" | custom-call | flops 6442450944 | bytes 50331648 | tf_op jit(solution)/shard_map/update/pallas_call | solution.py:303
Async XLA Ops:
  0.0 0.8 copy-start
  0.8 0.7 copy-start.1
  1.5 0.7 copy-start.2
  15.8 0.7 copy-start.3
  48.2 102.2 %copy-start.4 = (s32[32]{0:T(128)S(1)}, s32[32]{0:T(128)}, u32[]{:S(2)}) copy-start(s32[32]{0:T(128)} %order_ref.3) | copy-start | bytes 388
